TPU v7x, 32 devices: a whole 2x2x4 slice. The times are simulated.
32 devices in a mesh: subj: 8 (over z, y), slab: 4 (over x, core).
Axes of the slice: x: 2, y: 2, z: 4, core: 2. Of those that a mesh axis runs over, the one named last changes fastest.
Arguments:
- fod: bfloat16 [32, 45, 2048], P('subj', None, 'slab'), may hold values from -24 to 24
- rotation: bfloat16 [32, 45, 45, 2048], P('subj', None, None, 'slab'), may hold values from -0.875 to 0.875
- modulation: float32 [32, 2048], P('subj', 'slab'), may hold values from 0.3 to 3
- subject_ids: int32 [32], P('subj'), may hold values from 0 to 31, each once
- subject_weight: float32 [32], replicated, may hold values from 0.5 to 2
- voxel_cell_index: int32 [2048], P('slab'), may hold values from 0 to 1023, as said below
Outputs:
- template: bfloat16 [45, 4096], replicated
Inputs may be any that keep to these rules, and one draw needn't show every extreme that they name: `voxel_cell_index`: within each aligned block of 512 entries (one slab's masked voxels) the cell numbers are distinct and increasing.
All inputs are finite; a program needn't handle non-finite values.
Results may differ from a plain program's by a relative error of at most 0.001.
Values may be sent and summed in bfloat16 or wider, within the bound.
No kernel may reach another device: no remote copies, remote signals or barrier semaphores. Data moves between devices by JAX's collectives and lax.ppermute only.
A program may use at most 64 MiB of HBM per device.

v0:
```python
import jax
import jax.numpy as jnp
from jax import lax
from jax.sharding import PartitionSpec as P

GRID_DEV = 1024


def on_device(fod, rotation, modulation, subject_ids, subject_weight, voxel_cell_index):
    total_subjects = subject_weight.shape[0]
    indicator_rows = (
        subject_ids[:, None] == jnp.arange(total_subjects, dtype=jnp.int32)[None, :]
    ).astype(jnp.float32)
    selected_cells = jnp.dot(indicator_rows, subject_weight, precision=lax.Precision.HIGHEST)
    weight = modulation * selected_cells[:, None]
    rotated_coefficients = jnp.einsum(
        "xfhu,xhu->xfu", rotation, fod, preferred_element_type=jnp.float32
    )
    numer = jnp.sum(rotated_coefficients * weight[:, None, :], axis=0)
    denom = jnp.sum(weight, axis=0)
    numer, denom = lax.psum((numer, denom), "subj")
    average = (numer / denom[None, :]).astype(jnp.bfloat16)
    dense = jnp.zeros((average.shape[0], GRID_DEV), jnp.bfloat16)
    dense = dense.at[:, voxel_cell_index].set(average)
    return lax.all_gather(dense, "slab", axis=1, tiled=True)


def solution(mesh):
    placed = (
        P("subj", None, "slab"),
        P("subj", None, None, "slab"),
        P("subj", "slab"),
        P("subj"),
        P(),
        P("slab"),
    )
    return jax.shard_map(on_device, mesh=mesh, in_specs=placed, out_specs=P(), check_vma=False)
```

profile of v0, /device:TPU:0, one launch (start us, length us, event | category | flops | bytes accessed | tf_op | source)
XLA Modules:
  0.0 111.8 jit_solution(3160087233603717276)
XLA Ops:
  6.5 0.0 copy-start
  6.5 0.0 copy-start.1
  6.5 0.0 all-reduce.2.cloned.1.call-start
  6.5 1.0 bitcast_convert_fusion
  7.5 0.0 copy-done
  7.5 0.8 convolution_bitcast_fusion
  8.4 0.8 fusion.5
  9.2 7.8 %multiply_reduce_fusion = f32[4,512,45]{1,0,2:T(4,128)S(1)} fusion(f32[4,512,45]{1,0,2:T(4,128)S(1)} %bitcast_convert_fusion, bf16[4,45,45,512]{3,0,2,1:T(4,128)(2,1)} %param.7), kind=kLoop, calls=%fused_computation.1 | loop fusion | flops 12349440 | bytes 9031680 | tf_op jit(solution)/shard_map/xfhu,xhu->xfu/dot_general | solution.py:16
  16.9 0.9 multiply_reduce_fusion.1
  17.8 0.0 all-reduce.2.cloned.1.call-update
  17.8 0.0 copy-done.1
  17.9 23.3 %psum.15 = f32[512]{0:T(512)S(1)} all-reduce(f32[512]{0:T(512)S(1)} %get-tuple-element.5), channel_id=1, replica_groups=mesh['subj'=8,'slab'=4] {'subj'}, use_global_device_ids=true, to_apply=%region_3.0 | all-reduce | flops 512 | bytes 4096 | tf_op jit(solution)/shard_map/psum | solution.py:21
  41.1 49.8 %all-reduce.2.cloned.1.call-done = f32[45,512]{1,0:T(8,128)} async-done(((f32[45,512]{1,0:T(8,128)}), f32[45,512]{1,0:T(8,128)}) %all-reduce.2.cloned.1.call-update) | async-done | bytes 92176 | tf_op jit(solution)/shard_map/psum | solution.py:21
  90.9 0.9 fusion.2
  91.8 0.1 copy.8
  92.0 1.8 %scatter_custom_fusion = bf16[45,1024]{0,1:T(8,128)(2,1)S(1)} fusion(s32[512]{0:T(512)S(1)} %compare_select_fusion, bf16[512,45]{1,0:T(8,128)(2,1)S(1)} %copy.8, bf16[]{:T(256)} %constant.0.clone.1), kind=kCustom, calls=%fused_computation.5 | custom fusion | bytes 92162 | tf_op jit(solution)/shard_map/scatter | solution.py:24
  93.8 10.0 %all_gather.3 = bf16[45,4096]{0,1:T(8,128)(2,1)S(1)} all-gather(bf16[45,1024]{0,1:T(8,128)(2,1)S(1)} %scatter_custom_fusion), channel_id=1, replica_groups=mesh['subj'=8,'slab'=4] {'slab'}, dimensions={1}, use_global_device_ids=true | all-gather | bytes 460800 | tf_op jit(solution)/shard_map/all_gather | solution.py:25
  103.8 1.2 %copy.9 = bf16[45,4096]{1,0:T(8,128)(2,1)} copy(bf16[45,4096]{0,1:T(8,128)(2,1)S(1)} %all_gather.3) | data formatting | bytes 737280 | tf_op jit(solution)/shard_map/all_gather | solution.py:25
  (1 shorter events, 0.0 us)
Async XLA Ops:
  6.5 1.0 copy-start
  6.5 11.3 %copy-start.1 = (s32[512]{0:T(512)S(1)}, s32[512]{0:T(512)}, u32[]{:S(2)}) copy-start(s32[512]{0:T(512)} %param.11) | copy-start | bytes 6148
  6.5 84.4 %all-reduce.2.cloned.1.call-start = ((), (), s32[]{:S(2)}) async-start(), calls=%async_computation | async-start | bytes 196608 | tf_op jit(solution)/shard_map/psum | solution.py:21
Sparse Core Ops, SparseCore 0:
  18.0 72.8 all-reduce.1
where the time goes:
time: 112 us
  waiting for transfers between devices  49.8 us (44%)
  blocking collectives  33.3 us (30%)
  between operations  13.4 us (12%)
  other arithmetic  11.3 us (10%)
  local copies, waits for them, and re-layouts  3.16 us (3%)
    psum x1, waiting for transfers between devices, on_device(): numer, denom = lax.psum((numer, denom), 'subj')  49.8 us
    psum x1, blocking collectives, on_device(): numer, denom = lax.psum((numer, denom), 'subj')  23.3 us
    all_gather x1, blocking collectives, on_device(): return lax.all_gather(dense, 'slab', axis=1, tiled=True)  10 us
    dot_general x1, other arithmetic, on_device(): jnp.einsum('xfhu,xhu->xfu', rotation, fod, preferred_element_type=jnp.flo...  7.78 us
  transfers between devices with their start and end apart: 1, of which 1 were waited for; matrix products, arithmetic and copies ran while one was open for 0% of the time, Pallas kernels for 0%

commit v1 on v0

v1 whole, which is shorter than its diff:
```python
import jax
import jax.numpy as jnp
from jax import lax
from jax.sharding import PartitionSpec as P

GRID_DEV = 1024


def exchange(value, axis, size, bit):
    return lax.ppermute(value, axis, [(i, i ^ bit) for i in range(size)])


def butterfly_sum(value, axis, size):
    if size & (size - 1):
        return lax.psum(value, axis)
    bit = 1
    while bit < size:
        value = value + exchange(value, axis, size, bit)
        bit *= 2
    return value


def butterfly_gather(value, axis, size):
    if size & (size - 1):
        return lax.all_gather(value, axis, axis=1, tiled=True)
    index = lax.axis_index(axis)
    width = value.shape[1]
    bit = size // 2
    while bit:
        other = exchange(value, axis, size, bit)
        low = (index & bit) == 0
        first, second = jnp.where(low, value, other), jnp.where(low, other, value)
        blocks = []
        for start in range(0, value.shape[1], width):
            blocks += [first[:, start : start + width], second[:, start : start + width]]
        value = jnp.concatenate(blocks, axis=1)
        bit //= 2
    return value


def on_device(subj, slab, fod, rotation, modulation, subject_ids, subject_weight, voxel_cell_index):
    total_subjects = subject_weight.shape[0]
    coef = fod.shape[1]
    picked = subject_ids[:, None] == jnp.arange(total_subjects, dtype=jnp.int32)[None, :]
    weight = modulation * jnp.sum(jnp.where(picked, subject_weight[None, :], 0.0), axis=1)[:, None]
    weighted_fod = fod.astype(jnp.float32) * weight[:, None, :]
    numer = jnp.sum(rotation.astype(jnp.float32) * weighted_fod[:, None], axis=(0, 2))
    sums = jnp.concatenate([numer, jnp.sum(weight, axis=0)[None]], axis=0)
    sums = butterfly_sum(sums, "subj", subj)
    average = (sums[:coef] / sums[coef:]).astype(jnp.bfloat16)
    onehot = (voxel_cell_index[:, None] == jnp.arange(GRID_DEV, dtype=jnp.int32)[None, :]).astype(jnp.bfloat16)
    dense = jnp.dot(average, onehot, preferred_element_type=jnp.float32).astype(jnp.bfloat16)
    return butterfly_gather(dense, "slab", slab)


def solution(mesh):
    placed = (
        P("subj", None, "slab"),
        P("subj", None, None, "slab"),
        P("subj", "slab"),
        P("subj"),
        P(),
        P("slab"),
    )
    subj, slab = mesh.shape["subj"], mesh.shape["slab"]

    def body(*args):
        return on_device(subj, slab, *args)

    return jax.shard_map(body, mesh=mesh, in_specs=placed, out_specs=P(), check_vma=False)
```

time: 112 us -> 34.7 us (0.31)
  waiting for transfers between devices: 49.8 us -> 12.4 us
  blocking collectives: 33.3 us -> 0 us
  between operations: 13.4 us -> 0.09 us
  starting transfers between devices: 0.01 us -> 9.9 us
  local copies, waits for them, and re-layouts: 3.16 us -> 0.04 us
    psum x1 -> x0, waiting for transfers between devices: 49.8 us -> none  [on_device(): numer, denom = lax.psum((numer, denom), 'subj')]
    psum x1 -> x0, blocking collectives: 23.3 us -> none  [on_device(): numer, denom = lax.psum((numer, denom), 'subj')]
    ppermute x0 -> x5, waiting for transfers between devices: none -> 12.4 us  [exchange(): return lax.ppermute(value, axis, [(i, i ^ bit) for i in range(size)])]
    all_gather x1 -> x0, blocking collectives: 10 us -> none  [on_device(): return lax.all_gather(dense, 'slab', axis=1, tiled=True)]
    ppermute x0 -> x5, starting transfers between devices: none -> 9.9 us  [exchange(): return lax.ppermute(value, axis, [(i, i ^ bit) for i in range(size)])]
    dot_general x1 -> x0, other arithmetic: 7.78 us -> none  [on_device(): jnp.einsum('xfhu,xhu->xfu', rotation, fod, preferred_element_type=jnp.flo...]
    reduce_sum x2 -> x3, other arithmetic: 1.67 us -> 9.44 us  [the longest x1 7.79 us: on_device(): jnp.sum(rotation.astype(jnp.float32) * weighted_fod[:, None], axis=(0, 2))]
    scatter x1 -> x0, local copies, waits for them, and re-layouts: 1.83 us -> none  [on_device(): dense = dense.at[:, voxel_cell_index].set(average)]
  transfers between devices with their start and end apart: 1 -> 5, of which waited for: 1 -> 5; matrix products, arithmetic and copies ran while one was open for 0% -> 0% of each run, Pallas kernels for 0% -> 0%
where the time goes in v1:
time: 34.7 us; the launch traced here: 34.4 us
  waiting for transfers between devices  12.4 us (36%)
  other arithmetic  11.4 us (33%)
  starting transfers between devices  9.9 us (29%)
  matrix products  0.57 us (2%)
    ppermute x5, waiting for transfers between devices, exchange(): return lax.ppermute(value, axis, [(i, i ^ bit) for i in range(size)])  12.4 us
    ppermute x5, starting transfers between devices, exchange(): return lax.ppermute(value, axis, [(i, i ^ bit) for i in range(size)])  9.9 us
    reduce_sum x1, other arithmetic, on_device(): jnp.sum(rotation.astype(jnp.float32) * weighted_fod[:, None], axis=(0, 2))  7.79 us
    mul x1, other arithmetic, on_device(): weighted_fod = fod.astype(jnp.float32) * weight[:, None, :]  0.99 us
    reduce_sum x1, other arithmetic, on_device(): jnp.sum(jnp.where(picked, subject_weight[None, :], 0.0), axis=1)[:, None]  0.86 us
    concatenate x2, other arithmetic, butterfly_gather(): value = jnp.concatenate(blocks, axis=1)  0.79 us
    reduce_sum x1, other arithmetic, on_device(): sums = jnp.concatenate([numer, jnp.sum(weight, axis=0)[None]], axis=0)  0.78 us
  transfers between devices with their start and end apart: 5, of which 5 were waited for; matrix products, arithmetic and copies ran while one was open for 0% of the time, Pallas kernels for 0%

profile of v1, /device:TPU:0, one launch (start us, length us, event | category | flops | bytes accessed | tf_op | source)
XLA Modules:
  0.0 34.4 jit_solution(13881705059786963080)
XLA Ops:
  0.0 0.0 copy-start
  0.0 0.9 %select_reduce_fusion = f32[4]{0:T(128)S(1)} fusion(f32[32]{0:T(128)} %param.10, s32[4]{0:T(128)} %param.9), kind=kLoop, calls=%fused_computation.17 | loop fusion | flops 380 | bytes 160 | tf_op jit(solution)/shard_map/reduce_sum | solution.py:45
  0.9 0.8 %fusion.6 = (f32[512]{0:T(512)S(1)}, f32[4,512]{1,0:T(4,128)S(1)}) fusion(f32[4,512]{1,0:T(4,128)} %param.8, f32[4]{0:T(128)S(1)} %select_reduce_fusion), kind=kLoop, calls=%fused_computation.19 | loop fusion | flops 3584 | bytes 18448 | tf_op jit(solution)/shard_map/reduce_sum | solution.py:48
  1.7 1.0 %convert_multiply_fusion = f32[4,45,512]{2,0,1:T(4,128)S(1)} fusion(bf16[4,45,512]{2,0,1:T(4,128)(2,1)} %param.6, f32[4,512]{1,0:T(4,128)S(1)} %get-tuple-element.6), kind=kLoop, calls=%fused_computation.6 | loop fusion | flops 184320 | bytes 561152 | tf_op jit(solution)/shard_map/mul | solution.py:46
  2.6 7.8 %multiply_reduce_fusion = f32[45,512]{1,0:T(8,128)S(1)} fusion(bf16[4,45,45,512]{3,0,2,1:T(4,128)(2,1)} %param.7, f32[4,45,512]{2,0,1:T(4,128)S(1)} %convert_multiply_fusion), kind=kLoop, calls=%fused_computation | loop fusion | flops 12418560 | bytes 8755200 | tf_op jit(solution)/shard_map/reduce_sum | solution.py:47
  10.5 3.1 %collective-permute-start = (f32[46,512]{1,0:T(8,128)S(1)}, f32[46,512]{1,0:T(8,128)S(1)}, u32[]{:S(2)}, u32[]{:S(2)}) collective-permute-start(f32[46,512]{1,0:T(8,128)S(1)} %pad_maximum_fusion.2), channel_id=1, source_target_pairs={{0,4},{4,0},{8,12},{12,8},{16,20},{20,16},{24,28},{28,24},{1,5},{5... | collective-permute-start | bytes 282632 | tf_op jit(solution)/shard_map/ppermute | solution.py:10
  13.5 2.8 %collective-permute-done = f32[46,512]{1,0:T(8,128)S(1)} collective-permute-done((f32[46,512]{1,0:T(8,128)S(1)}, f32[46,512]{1,0:T(8,128)S(1)}, u32[]{:S(2)}, u32[]{:S(2)}) %collective-permute-start) | collective-permute-done | bytes 94240 | tf_op jit(solution)/shard_map/ppermute | solution.py:10
  16.3 1.9 %collective-permute-start.1 = (f32[46,512]{1,0:T(8,128)S(1)}, f32[46,512]{1,0:T(8,128)S(1)}, u32[]{:S(2)}, u32[]{:S(2)}) collective-permute-start(f32[46,512]{1,0:T(8,128)S(1)} %fusion.9), channel_id=1, source_target_pairs={{0,8},{4,12},{8,0},{12,4},{16,24},{20,28},{24,16},{28,20},{1,9},{5... | collective-permute-start | bytes 282632 | tf_op jit(solution)/shard_map/ppermute | solution.py:10
  18.3 2.7 %collective-permute-done.1 = f32[46,512]{1,0:T(8,128)S(1)} collective-permute-done((f32[46,512]{1,0:T(8,128)S(1)}, f32[46,512]{1,0:T(8,128)S(1)}, u32[]{:S(2)}, u32[]{:S(2)}) %collective-permute-start.1) | collective-permute-done | bytes 94240 | tf_op jit(solution)/shard_map/ppermute | solution.py:10
  21.0 3.0 %collective-permute-start.2 = (f32[46,512]{1,0:T(8,128)S(1)}, f32[46,512]{1,0:T(8,128)S(1)}, u32[]{:S(2)}, u32[]{:S(2)}) collective-permute-start(f32[46,512]{1,0:T(8,128)S(1)} %add.10), channel_id=1, source_target_pairs={{0,16},{4,20},{8,24},{12,28},{16,0},{20,4},{24,8},{28,12},{1,17},{... | collective-permute-start | bytes 282632 | tf_op jit(solution)/shard_map/ppermute | solution.py:10
  24.0 2.6 %collective-permute-done.2 = f32[46,512]{1,0:T(8,128)S(1)} collective-permute-done((f32[46,512]{1,0:T(8,128)S(1)}, f32[46,512]{1,0:T(8,128)S(1)}, u32[]{:S(2)}, u32[]{:S(2)}) %collective-permute-start.2) | collective-permute-done | bytes 94240 | tf_op jit(solution)/shard_map/ppermute | solution.py:10
  26.6 0.0 copy-done
  26.7 0.6 %fusion.1 = bf16[45,1024]{1,0:T(8,128)(2,1)S(1)} fusion(s32[512]{0:T(512)S(1)} %copy-done, f32[46,512]{1,0:T(8,128)S(1)} %add.11, f32[512]{0:T(512)S(1)} %bitcast.4), kind=kOutput, calls=%fused_computation.3 | convolution fusion | flops 47802368 | bytes 190464 | tf_op jit(solution)/shard_map/dot_general | solution.py:52
  27.2 1.9 %collective-permute-start.3 = (bf16[45,1024]{1,0:T(8,128)(2,1)S(1)}, bf16[45,1024]{1,0:T(8,128)(2,1)S(1)}, u32[]{:S(2)}, u32[]{:S(2)}) collective-permute-start(bf16[45,1024]{1,0:T(8,128)(2,1)S(1)} %fusion.1), channel_id=1, source_target_pairs={{0,2},{1,3},{2,0},{3,1},{4,6},{5,7},{6,4},{7,5},{8,10},{9,11},{10,... | collective-permute-start | bytes 276488 | tf_op jit(solution)/shard_map/ppermute | solution.py:10
  29.1 2.8 %collective-permute-done.3 = bf16[45,1024]{1,0:T(8,128)(2,1)S(1)} collective-permute-done((bf16[45,1024]{1,0:T(8,128)(2,1)S(1)}, bf16[45,1024]{1,0:T(8,128)(2,1)S(1)}, u32[]{:S(2)}, u32[]{:S(2)}) %collective-permute-start.3) | collective-permute-done | bytes 92192 | tf_op jit(solution)/shard_map/ppermute | solution.py:10
  32.0 0.1 collective-permute-start.4
  32.0 1.4 %collective-permute-done.4 = bf16[45,2048]{1,0:T(8,128)(2,1)S(1)} collective-permute-done((bf16[45,2048]{1,0:T(8,128)(2,1)S(1)}, bf16[45,2048]{1,0:T(8,128)(2,1)S(1)}, u32[]{:S(2)}, u32[]{:S(2)}) %collective-permute-start.4) | collective-permute-done | bytes 184352 | tf_op jit(solution)/shard_map/ppermute | solution.py:10
  33.5 0.1 broadcast_select_fusion.1
  33.6 0.8 %pad_maximum_fusion = bf16[45,4096]{1,0:T(8,128)(2,1)} fusion(bf16[45,1024]{1,0:T(8,128)(2,1)S(1)} %get-tuple-element.15, bf16[45,1024]{1,0:T(8,128)(2,1)S(1)} %get-tuple-element.10, bf16[45,1024]{1,0:T(8,128)(2,1)S(1)} %get-tuple-element.16, bf16[45,1024]{1,0:T(8,128)(2,1)S(1)} %get-tuple-element.9), kind=kLoop, calls=%fused_computation.5 | loop fusion | flops 1474560 | bytes 737280 | tf_op jit(solution)/shard_map/concatenate | solution.py:36
  (8 shorter events, 0.1 us)
Async XLA Ops:
  0.0 26.6 %copy-start = (s32[512]{0:T(512)S(1)}, s32[512]{0:T(512)}, u32[]{:S(2)}) copy-start(s32[512]{0:T(512)} %param.11) | copy-start | bytes 6148
  10.5 5.9 %collective-permute-start = (f32[46,512]{1,0:T(8,128)S(1)}, f32[46,512]{1,0:T(8,128)S(1)}, u32[]{:S(2)}, u32[]{:S(2)}) collective-permute-start(f32[46,512]{1,0:T(8,128)S(1)} %pad_maximum_fusion.2), channel_id=1, source_target_pairs={{0,4},{4,0},{8,12},{12,8},{16,20},{20,16},{24,28},{28,24},{1,5},{5... | collective-permute-start | bytes 282632 | tf_op jit(solution)/shard_map/ppermute | solution.py:10
  16.3 4.7 %collective-permute-start.1 = (f32[46,512]{1,0:T(8,128)S(1)}, f32[46,512]{1,0:T(8,128)S(1)}, u32[]{:S(2)}, u32[]{:S(2)}) collective-permute-start(f32[46,512]{1,0:T(8,128)S(1)} %fusion.9), channel_id=1, source_target_pairs={{0,8},{4,12},{8,0},{12,4},{16,24},{20,28},{24,16},{28,20},{1,9},{5... | collective-permute-start | bytes 282632 | tf_op jit(solution)/shard_map/ppermute | solution.py:10
  21.0 5.6 %collective-permute-start.2 = (f32[46,512]{1,0:T(8,128)S(1)}, f32[46,512]{1,0:T(8,128)S(1)}, u32[]{:S(2)}, u32[]{:S(2)}) collective-permute-start(f32[46,512]{1,0:T(8,128)S(1)} %add.10), channel_id=1, source_target_pairs={{0,16},{4,20},{8,24},{12,28},{16,0},{20,4},{24,8},{28,12},{1,17},{... | collective-permute-start | bytes 282632 | tf_op jit(solution)/shard_map/ppermute | solution.py:10
  27.2 4.7 %collective-permute-start.3 = (bf16[45,1024]{1,0:T(8,128)(2,1)S(1)}, bf16[45,1024]{1,0:T(8,128)(2,1)S(1)}, u32[]{:S(2)}, u32[]{:S(2)}) collective-permute-start(bf16[45,1024]{1,0:T(8,128)(2,1)S(1)} %fusion.1), channel_id=1, source_target_pairs={{0,2},{1,3},{2,0},{3,1},{4,6},{5,7},{6,4},{7,5},{8,10},{9,11},{10,... | collective-permute-start | bytes 276488 | tf_op jit(solution)/shard_map/ppermute | solution.py:10
  32.0 1.5 %collective-permute-start.4 = (bf16[45,2048]{1,0:T(8,128)(2,1)S(1)}, bf16[45,2048]{1,0:T(8,128)(2,1)S(1)}, u32[]{:S(2)}, u32[]{:S(2)}) collective-permute-start(bf16[45,2048]{1,0:T(8,128)(2,1)S(1)} %pad_maximum_fusion.1), channel_id=1, source_target_pairs={{0,1},{1,0},{2,3},{3,2},{4,5},{5,4},{6,7},{7,6},{8,9},{9,8},{10,11... | collective-permute-start | bytes 552968 | tf_op jit(solution)/shard_map/ppermute | solution.py:10

commit v2 on v1

--- a/solution.py
+++ b/solution.py
@@ -1,9 +1,14 @@
+import functools
+
 import jax
 import jax.numpy as jnp
 from jax import lax
+from jax.experimental import pallas as pl
+from jax.experimental.pallas import tpu as pltpu
 from jax.sharding import PartitionSpec as P
 
 GRID_DEV = 1024
+LANES = 128
 
 
 def exchange(value, axis, size, bit):
@@ -38,15 +43,104 @@
     return value
 
 
+def sums_kernel(
+    subjects,
+    chunk,
+    rotation_hbm,
+    fod_hbm,
+    modulation_hbm,
+    ids_hbm,
+    study_hbm,
+    out_ref,
+    rotation,
+    fod,
+    modulation,
+    ids,
+    study,
+    weighted,
+    partial,
+    big_sem,
+    small_sem,
+):
+    coef, _, rows, _ = rotation.shape
+    small = [
+        pltpu.make_async_copy(ids_hbm, ids, small_sem.at[0]),
+        pltpu.make_async_copy(study_hbm, study, small_sem.at[1]),
+        pltpu.make_async_copy(modulation_hbm, modulation, small_sem.at[2]),
+        pltpu.make_async_copy(fod_hbm, fod, small_sem.at[3]),
+    ]
+    for copy in small:
+        copy.start()
+
+    def big(step):
+        part = pl.ds(step * chunk, chunk)
+        return pltpu.make_async_copy(rotation_hbm.at[part], rotation.at[part], big_sem.at[step])
+
+    for step in range(coef // chunk):
+        big(step).start()
+    for copy in small:
+        copy.wait()
+
+    subject = lax.broadcasted_iota(jnp.int32, (rows, LANES), 0) % subjects
+    factor = jnp.zeros((rows, LANES), jnp.float32)
+    for s in range(subjects):
+        factor = jnp.where(subject == s, study[ids[s]], factor)
+    weight = modulation[...] * factor
+    partial[pl.ds(coef * rows, rows)] = weight
+    for k in range(coef):
+        weighted[k] = fod[k].astype(jnp.float32) * weight
+
+    @pl.loop(0, coef // chunk)
+    def _(step):
+        big(step).wait()
+        total = [jnp.zeros((rows, LANES), jnp.float32) for _ in range(chunk)]
+        for k in range(coef):
+            term = weighted[k]
+            for c in range(chunk):
+                total[c] += rotation[step * chunk + c, k].astype(jnp.float32) * term
+        for c in range(chunk):
+            partial[pl.ds(pl.multiple_of((step * chunk + c) * rows, rows), rows)] = total[c]
+
+    count = out_ref.shape[0]
+    out = partial[pl.ds(0, count, stride=subjects)]
+    for s in range(1, subjects):
+        out += partial[pl.ds(s, count, stride=subjects)]
+    out_ref[...] = out
+
+
+def local_sums(fod, rotation, modulation, subject_ids, subject_weight):
+    subjects, coef, voxels = fod.shape
+    blocks = voxels // LANES
+    rows = blocks * subjects
+    chunk = next(n for n in (5, 4, 3, 2, 1) if coef % n == 0)
+    turned = rotation.transpose(1, 2, 0, 3).reshape(coef, coef, subjects, blocks, LANES)
+    turned = turned.transpose(0, 1, 3, 2, 4).reshape(coef, coef, rows, LANES)
+    fod = fod.transpose(1, 0, 2).reshape(coef, subjects, blocks, LANES).transpose(0, 2, 1, 3).reshape(coef, rows, LANES)
+    modulation = modulation.reshape(subjects, blocks, LANES).transpose(1, 0, 2).reshape(rows, LANES)
+    return pl.pallas_call(
+        functools.partial(sums_kernel, subjects, chunk),
+        out_shape=jax.ShapeDtypeStruct(((coef + 1) * blocks, LANES), jnp.float32),
+        in_specs=[pl.BlockSpec(memory_space=pl.ANY)] * 5,
+        out_specs=pl.BlockSpec(memory_space=pltpu.VMEM),
+        scratch_shapes=[
+            pltpu.VMEM(turned.shape, turned.dtype),
+            pltpu.VMEM(fod.shape, fod.dtype),
+            pltpu.VMEM(modulation.shape, jnp.float32),
+            pltpu.SMEM(subject_ids.shape, jnp.int32),
+            pltpu.SMEM(subject_weight.shape, jnp.float32),
+            pltpu.VMEM(fod.shape, jnp.float32),
+            pltpu.VMEM(((coef + 1) * rows, LANES), jnp.float32),
+            pltpu.SemaphoreType.DMA((coef // chunk,)),
+            pltpu.SemaphoreType.DMA((4,)),
+        ],
+        name="local_sums",
+    )(turned, fod, modulation, subject_ids, subject_weight)
+
+
 def on_device(subj, slab, fod, rotation, modulation, subject_ids, subject_weight, voxel_cell_index):
-    total_subjects = subject_weight.shape[0]
-    coef = fod.shape[1]
-    picked = subject_ids[:, None] == jnp.arange(total_subjects, dtype=jnp.int32)[None, :]
-    weight = modulation * jnp.sum(jnp.where(picked, subject_weight[None, :], 0.0), axis=1)[:, None]
-    weighted_fod = fod.astype(jnp.float32) * weight[:, None, :]
-    numer = jnp.sum(rotation.astype(jnp.float32) * weighted_fod[:, None], axis=(0, 2))
-    sums = jnp.concatenate([numer, jnp.sum(weight, axis=0)[None]], axis=0)
-    sums = butterfly_sum(sums, "subj", subj)
+    coef, voxels = fod.shape[1:]
+    sums = local_sums(fod, rotation, modulation, subject_ids, subject_weight)
+    sums = butterfly_sum(sums, "subj", subj).reshape(coef + 1, voxels)
     average = (sums[:coef] / sums[coef:]).astype(jnp.bfloat16)
     onehot = (voxel_cell_index[:, None] == jnp.arange(GRID_DEV, dtype=jnp.int32)[None, :]).astype(jnp.bfloat16)
     dense = jnp.dot(average, onehot, preferred_element_type=jnp.float32).astype(jnp.bfloat16)

time: 34.7 us -> 31.1 us (0.90)
  other arithmetic: 11.4 us -> 1.81 us
  Pallas kernels: 0 us -> 6 us
    reduce_sum x3 -> x0, other arithmetic: 9.44 us -> none  [the longest x1 7.79 us: on_device(): jnp.sum(rotation.astype(jnp.float32) * weighted_fod[:, None], axis=(0, 2))]
    pallas_call x0 -> x1, Pallas kernels: none -> 6 us  [local_sums(): pl.pallas_call(functools.partial(sums_kernel, subjects, chunk), out_shape...]
    mul x1 -> x0, other arithmetic: 0.99 us -> none  [on_device(): weighted_fod = fod.astype(jnp.float32) * weight[:, None, :]]
    add x3, other arithmetic: 0.05 us -> 0.93 us  [butterfly_sum(): value = value + exchange(value, axis, size, bit)]
where the time goes in v2:
time: 31.1 us; the launch traced here: 30.9 us
  waiting for transfers between devices  12.3 us (40%)
  starting transfers between devices  10 us (32%)
  Pallas kernels  6 us (19%)
  other arithmetic  1.81 us (6%)
  matrix products  0.57 us (2%)
    ppermute x5, waiting for transfers between devices, exchange(): return lax.ppermute(value, axis, [(i, i ^ bit) for i in range(size)])  12.3 us
    ppermute x5, starting transfers between devices, exchange(): return lax.ppermute(value, axis, [(i, i ^ bit) for i in range(size)])  10 us
    pallas_call x1, Pallas kernels, local_sums(): pl.pallas_call(functools.partial(sums_kernel, subjects, chunk), out_shape...  6 us
    add x3, other arithmetic, butterfly_sum(): value = value + exchange(value, axis, size, bit)  0.93 us
    concatenate x2, other arithmetic, butterfly_gather(): value = jnp.concatenate(blocks, axis=1)  0.79 us
  transfers between devices with their start and end apart: 5, of which 5 were waited for; matrix products, arithmetic and copies ran while one was open for 0% of the time, Pallas kernels for 0%

profile of v2, /device:TPU:0, one launch (start us, length us, event | category | flops | bytes accessed | tf_op | source)
XLA Modules:
  0.0 30.9 jit_solution(12196688116589526418)
XLA Ops:
  0.0 0.0 copy-start
  0.0 6.0 %local_sums.1 = f32[184,128]{1,0:T(8,128)} custom-call(bf16[45,45,16,128]{3,2,1,0:T(8,128)(2,1)} %bitcast.22, bf16[45,16,128]{2,1,0:T(8,128)(2,1)} %bitcast.24, f32[16,128]{1,0:T(8,128)} %bitcast.25, s32[4]{0:T(128)} %ids_hbm.1, f32[32]{0:T(128)} %study_hbm.1), custom_call_target="tpu_custom_call" | custom-call | tf_op jit(solution)/shard_map/local_sums/pallas_call | solution.py:120
  6.0 3.1 %collective-permute-start = (f32[184,128]{1,0:T(8,128)}, f32[184,128]{1,0:T(8,128)S(1)}, u32[]{:S(2)}, u32[]{:S(2)}) collective-permute-start(f32[184,128]{1,0:T(8,128)} %local_sums.1), channel_id=1, source_target_pairs={{0,4},{4,0},{8,12},{12,8},{16,20},{20,16},{24,28},{28,24},{1,5},{5... | collective-permute-start | bytes 282632 | tf_op jit(solution)/shard_map/ppermute | solution.py:15
  9.1 2.9 %collective-permute-done = f32[184,128]{1,0:T(8,128)S(1)} collective-permute-done((f32[184,128]{1,0:T(8,128)}, f32[184,128]{1,0:T(8,128)S(1)}, u32[]{:S(2)}, u32[]{:S(2)}) %collective-permute-start) | collective-permute-done | bytes 94240 | tf_op jit(solution)/shard_map/ppermute | solution.py:15
  12.0 0.9 %add.9 = f32[184,128]{1,0:T(8,128)S(1)} add(f32[184,128]{1,0:T(8,128)} %local_sums.1, f32[184,128]{1,0:T(8,128)S(1)} %collective-permute-done) | non-fusion elementwise | flops 23552 | bytes 282624 | tf_op jit(solution)/shard_map/add | solution.py:23
  12.9 2.0 %collective-permute-start.1 = (f32[184,128]{1,0:T(8,128)S(1)}, f32[184,128]{1,0:T(8,128)S(1)}, u32[]{:S(2)}, u32[]{:S(2)}) collective-permute-start(f32[184,128]{1,0:T(8,128)S(1)} %add.9), channel_id=1, source_target_pairs={{0,8},{4,12},{8,0},{12,4},{16,24},{20,28},{24,16},{28,20},{1,9},{5... | collective-permute-start | bytes 282632 | tf_op jit(solution)/shard_map/ppermute | solution.py:15
  14.9 2.6 %collective-permute-done.1 = f32[184,128]{1,0:T(8,128)S(1)} collective-permute-done((f32[184,128]{1,0:T(8,128)S(1)}, f32[184,128]{1,0:T(8,128)S(1)}, u32[]{:S(2)}, u32[]{:S(2)}) %collective-permute-start.1) | collective-permute-done | bytes 94240 | tf_op jit(solution)/shard_map/ppermute | solution.py:15
  17.5 3.0 %collective-permute-start.2 = (f32[184,128]{1,0:T(8,128)S(1)}, f32[184,128]{1,0:T(8,128)S(1)}, u32[]{:S(2)}, u32[]{:S(2)}) collective-permute-start(f32[184,128]{1,0:T(8,128)S(1)} %add.10), channel_id=1, source_target_pairs={{0,16},{4,20},{8,24},{12,28},{16,0},{20,4},{24,8},{28,12},{1,17},{... | collective-permute-start | bytes 282632 | tf_op jit(solution)/shard_map/ppermute | solution.py:15
  20.5 2.6 %collective-permute-done.2 = f32[184,128]{1,0:T(8,128)S(1)} collective-permute-done((f32[184,128]{1,0:T(8,128)S(1)}, f32[184,128]{1,0:T(8,128)S(1)}, u32[]{:S(2)}, u32[]{:S(2)}) %collective-permute-start.2) | collective-permute-done | bytes 94240 | tf_op jit(solution)/shard_map/ppermute | solution.py:15
  23.1 0.0 copy-done
  23.2 0.6 %fusion.1 = bf16[45,1024]{1,0:T(8,128)(2,1)S(1)} fusion(s32[512]{0:T(512)S(1)} %copy-done, f32[45,512]{1,0:T(8,128)S(1)} %slice.23, f32[512]{0:T(512)S(1)} %slice_bitcast_fusion), kind=kOutput, calls=%fused_computation.2 | convolution fusion | flops 47802368 | bytes 188416 | tf_op jit(solution)/shard_map/dot_general | solution.py:146
  23.7 1.9 %collective-permute-start.3 = (bf16[45,1024]{1,0:T(8,128)(2,1)S(1)}, bf16[45,1024]{1,0:T(8,128)(2,1)S(1)}, u32[]{:S(2)}, u32[]{:S(2)}) collective-permute-start(bf16[45,1024]{1,0:T(8,128)(2,1)S(1)} %fusion.1), channel_id=1, source_target_pairs={{0,2},{1,3},{2,0},{3,1},{4,6},{5,7},{6,4},{7,5},{8,10},{9,11},{10,... | collective-permute-start | bytes 276488 | tf_op jit(solution)/shard_map/ppermute | solution.py:15
  25.6 2.8 %collective-permute-done.3 = bf16[45,1024]{1,0:T(8,128)(2,1)S(1)} collective-permute-done((bf16[45,1024]{1,0:T(8,128)(2,1)S(1)}, bf16[45,1024]{1,0:T(8,128)(2,1)S(1)}, u32[]{:S(2)}, u32[]{:S(2)}) %collective-permute-start.3) | collective-permute-done | bytes 92192 | tf_op jit(solution)/shard_map/ppermute | solution.py:15
  28.5 0.1 collective-permute-start.4
  28.5 1.4 %collective-permute-done.4 = bf16[45,2048]{1,0:T(8,128)(2,1)S(1)} collective-permute-done((bf16[45,2048]{1,0:T(8,128)(2,1)S(1)}, bf16[45,2048]{1,0:T(8,128)(2,1)S(1)}, u32[]{:S(2)}, u32[]{:S(2)}) %collective-permute-start.4) | collective-permute-done | bytes 184352 | tf_op jit(solution)/shard_map/ppermute | solution.py:15
  30.0 0.1 broadcast_select_fusion.1
  30.1 0.8 %pad_maximum_fusion = bf16[45,4096]{1,0:T(8,128)(2,1)} fusion(bf16[45,1024]{1,0:T(8,128)(2,1)S(1)} %get-tuple-element.13, bf16[45,1024]{1,0:T(8,128)(2,1)S(1)} %get-tuple-element.8, bf16[45,1024]{1,0:T(8,128)(2,1)S(1)} %get-tuple-element.14, bf16[45,1024]{1,0:T(8,128)(2,1)S(1)} %get-tuple-element.7), kind=kLoop, calls=%fused_computation.4 | loop fusion | flops 1474560 | bytes 737280 | tf_op jit(solution)/shard_map/concatenate | solution.py:41
  (7 shorter events, 0.1 us)
Async XLA Ops:
  0.0 23.1 %copy-start = (s32[512]{0:T(512)S(1)}, s32[512]{0:T(512)}, u32[]{:S(2)}) copy-start(s32[512]{0:T(512)} %param.11) | copy-start | bytes 6148
  6.0 6.0 %collective-permute-start = (f32[184,128]{1,0:T(8,128)}, f32[184,128]{1,0:T(8,128)S(1)}, u32[]{:S(2)}, u32[]{:S(2)}) collective-permute-start(f32[184,128]{1,0:T(8,128)} %local_sums.1), channel_id=1, source_target_pairs={{0,4},{4,0},{8,12},{12,8},{16,20},{20,16},{24,28},{28,24},{1,5},{5... | collective-permute-start | bytes 282632 | tf_op jit(solution)/shard_map/ppermute | solution.py:15
  12.9 4.6 %collective-permute-start.1 = (f32[184,128]{1,0:T(8,128)S(1)}, f32[184,128]{1,0:T(8,128)S(1)}, u32[]{:S(2)}, u32[]{:S(2)}) collective-permute-start(f32[184,128]{1,0:T(8,128)S(1)} %add.9), channel_id=1, source_target_pairs={{0,8},{4,12},{8,0},{12,4},{16,24},{20,28},{24,16},{28,20},{1,9},{5... | collective-permute-start | bytes 282632 | tf_op jit(solution)/shard_map/ppermute | solution.py:15
  17.5 5.6 %collective-permute-start.2 = (f32[184,128]{1,0:T(8,128)S(1)}, f32[184,128]{1,0:T(8,128)S(1)}, u32[]{:S(2)}, u32[]{:S(2)}) collective-permute-start(f32[184,128]{1,0:T(8,128)S(1)} %add.10), channel_id=1, source_target_pairs={{0,16},{4,20},{8,24},{12,28},{16,0},{20,4},{24,8},{28,12},{1,17},{... | collective-permute-start | bytes 282632 | tf_op jit(solution)/shard_map/ppermute | solution.py:15
  23.7 4.7 %collective-permute-start.3 = (bf16[45,1024]{1,0:T(8,128)(2,1)S(1)}, bf16[45,1024]{1,0:T(8,128)(2,1)S(1)}, u32[]{:S(2)}, u32[]{:S(2)}) collective-permute-start(bf16[45,1024]{1,0:T(8,128)(2,1)S(1)} %fusion.1), channel_id=1, source_target_pairs={{0,2},{1,3},{2,0},{3,1},{4,6},{5,7},{6,4},{7,5},{8,10},{9,11},{10,... | collective-permute-start | bytes 276488 | tf_op jit(solution)/shard_map/ppermute | solution.py:15
  28.5 1.5 %collective-permute-start.4 = (bf16[45,2048]{1,0:T(8,128)(2,1)S(1)}, bf16[45,2048]{1,0:T(8,128)(2,1)S(1)}, u32[]{:S(2)}, u32[]{:S(2)}) collective-permute-start(bf16[45,2048]{1,0:T(8,128)(2,1)S(1)} %pad_maximum_fusion.1), channel_id=1, source_target_pairs={{0,1},{1,0},{2,3},{3,2},{4,5},{5,4},{6,7},{7,6},{8,9},{9,8},{10,11... | collective-permute-start | bytes 552968 | tf_op jit(solution)/shard_map/ppermute | solution.py:15

commit v3 on v2

--- a/solution.py
+++ b/solution.py
@@ -77,7 +77,7 @@
         return pltpu.make_async_copy(rotation_hbm.at[part], rotation.at[part], big_sem.at[step])
 
     for step in range(coef // chunk):
-        big(step).start()
+        big(step).start(priority=1)
     for copy in small:
         copy.wait()
 
@@ -119,7 +119,7 @@
     modulation = modulation.reshape(subjects, blocks, LANES).transpose(1, 0, 2).reshape(rows, LANES)
     return pl.pallas_call(
         functools.partial(sums_kernel, subjects, chunk),
-        out_shape=jax.ShapeDtypeStruct(((coef + 1) * blocks, LANES), jnp.float32),
+        out_shape=pltpu.VMEM(((coef + 1) * blocks, LANES), jnp.float32),
         in_specs=[pl.BlockSpec(memory_space=pl.ANY)] * 5,
         out_specs=pl.BlockSpec(memory_space=pltpu.VMEM),
         scratch_shapes=[
@@ -133,8 +133,9 @@
             pltpu.SemaphoreType.DMA((coef // chunk,)),
             pltpu.SemaphoreType.DMA((4,)),
         ],
+        compiler_params=pltpu.CompilerParams(vmem_limit_bytes=32 << 20),
         name="local_sums",
-    )(turned, fod, modulation, subject_ids, subject_weight)
+    )(*[pltpu.with_memory_space_constraint(x, pltpu.HBM) for x in (turned, fod, modulation, subject_ids, subject_weight)])
 
 
 def on_device(subj, slab, fod, rotation, modulation, subject_ids, subject_weight, voxel_cell_index):

time: 31.1 us -> 27.8 us (0.89)
  Pallas kernels: 6 us -> 3.81 us
  other arithmetic: 1.81 us -> 0.92 us
    pallas_call x1, Pallas kernels: 6 us -> 3.81 us  [local_sums(): pl.pallas_call(functools.partial(sums_kernel, subjects, chunk), out_shape...]
    add x3, other arithmetic: 0.93 us -> 0.04 us  [butterfly_sum(): value = value + exchange(value, axis, size, bit)]
where the time goes in v3:
time: 27.8 us; the launch traced here: 27.6 us
  waiting for transfers between devices  12.1 us (44%)
  starting transfers between devices  10 us (36%)
  Pallas kernels  3.81 us (14%)
  other arithmetic  0.92 us (3%)
  matrix products  0.57 us (2%)
    ppermute x5, waiting for transfers between devices, exchange(): return lax.ppermute(value, axis, [(i, i ^ bit) for i in range(size)])  12.1 us
    ppermute x5, starting transfers between devices, exchange(): return lax.ppermute(value, axis, [(i, i ^ bit) for i in range(size)])  10 us
    pallas_call x1, Pallas kernels, local_sums(): pl.pallas_call(functools.partial(sums_kernel, subjects, chunk), out_shape...  3.81 us
    concatenate x2, other arithmetic, butterfly_gather(): value = jnp.concatenate(blocks, axis=1)  0.79 us
    dot_general x1, matrix products, on_device(): jnp.dot(average, onehot, preferred_element_type=jnp.float32)  0.57 us
  transfers between devices with their start and end apart: 5, of which 5 were waited for; matrix products, arithmetic and copies ran while one was open for 0% of the time, Pallas kernels for 0%

profile of v3, /device:TPU:0, one launch (start us, length us, event | category | flops | bytes accessed | tf_op | source)
XLA Modules:
  0.0 27.6 jit_solution(4022155271692464744)
XLA Ops:
  0.0 0.0 copy-start
  0.0 3.8 %local_sums.1 = f32[184,128]{1,0:T(8,128)S(1)} custom-call(bf16[45,45,16,128]{3,2,1,0:T(8,128)(2,1)} %bitcast.22, bf16[45,16,128]{2,1,0:T(8,128)(2,1)} %bitcast.24, f32[16,128]{1,0:T(8,128)} %bitcast.25, s32[4]{0:T(128)} %ids_hbm.1, f32[32]{0:T(128)} %study_hbm.1), custom_call_target="tpu_custom_call" | custom-call | tf_op jit(solution)/shard_map/local_sums/pallas_call | solution.py:120
  3.8 3.1 %collective-permute-start = (f32[184,128]{1,0:T(8,128)S(1)}, f32[184,128]{1,0:T(8,128)S(1)}, u32[]{:S(2)}, u32[]{:S(2)}) collective-permute-start(f32[184,128]{1,0:T(8,128)S(1)} %local_sums.1), channel_id=1, source_target_pairs={{0,4},{4,0},{8,12},{12,8},{16,20},{20,16},{24,28},{28,24},{1,5},{5... | collective-permute-start | bytes 282632 | tf_op jit(solution)/shard_map/ppermute | solution.py:15
  6.9 2.7 %collective-permute-done = f32[184,128]{1,0:T(8,128)S(1)} collective-permute-done((f32[184,128]{1,0:T(8,128)S(1)}, f32[184,128]{1,0:T(8,128)S(1)}, u32[]{:S(2)}, u32[]{:S(2)}) %collective-permute-start) | collective-permute-done | bytes 94240 | tf_op jit(solution)/shard_map/ppermute | solution.py:15
  9.6 2.0 %collective-permute-start.1 = (f32[184,128]{1,0:T(8,128)S(1)}, f32[184,128]{1,0:T(8,128)S(1)}, u32[]{:S(2)}, u32[]{:S(2)}) collective-permute-start(f32[184,128]{1,0:T(8,128)S(1)} %add.9), channel_id=1, source_target_pairs={{0,8},{4,12},{8,0},{12,4},{16,24},{20,28},{24,16},{28,20},{1,9},{5... | collective-permute-start | bytes 282632 | tf_op jit(solution)/shard_map/ppermute | solution.py:15
  11.6 2.6 %collective-permute-done.1 = f32[184,128]{1,0:T(8,128)S(1)} collective-permute-done((f32[184,128]{1,0:T(8,128)S(1)}, f32[184,128]{1,0:T(8,128)S(1)}, u32[]{:S(2)}, u32[]{:S(2)}) %collective-permute-start.1) | collective-permute-done | bytes 94240 | tf_op jit(solution)/shard_map/ppermute | solution.py:15
  14.3 3.0 %collective-permute-start.2 = (f32[184,128]{1,0:T(8,128)S(1)}, f32[184,128]{1,0:T(8,128)S(1)}, u32[]{:S(2)}, u32[]{:S(2)}) collective-permute-start(f32[184,128]{1,0:T(8,128)S(1)} %add.10), channel_id=1, source_target_pairs={{0,16},{4,20},{8,24},{12,28},{16,0},{20,4},{24,8},{28,12},{1,17},{... | collective-permute-start | bytes 282632 | tf_op jit(solution)/shard_map/ppermute | solution.py:15
  17.3 2.6 %collective-permute-done.2 = f32[184,128]{1,0:T(8,128)S(1)} collective-permute-done((f32[184,128]{1,0:T(8,128)S(1)}, f32[184,128]{1,0:T(8,128)S(1)}, u32[]{:S(2)}, u32[]{:S(2)}) %collective-permute-start.2) | collective-permute-done | bytes 94240 | tf_op jit(solution)/shard_map/ppermute | solution.py:15
  19.9 0.0 copy-done
  19.9 0.6 %fusion.1 = bf16[45,1024]{1,0:T(8,128)(2,1)S(1)} fusion(s32[512]{0:T(512)S(1)} %copy-done, f32[45,512]{1,0:T(8,128)S(1)} %slice.23, f32[512]{0:T(512)S(1)} %slice_bitcast_fusion), kind=kOutput, calls=%fused_computation.2 | convolution fusion | flops 47802368 | bytes 188416 | tf_op jit(solution)/shard_map/dot_general | solution.py:147
  20.4 1.9 %collective-permute-start.3 = (bf16[45,1024]{1,0:T(8,128)(2,1)S(1)}, bf16[45,1024]{1,0:T(8,128)(2,1)S(1)}, u32[]{:S(2)}, u32[]{:S(2)}) collective-permute-start(bf16[45,1024]{1,0:T(8,128)(2,1)S(1)} %fusion.1), channel_id=1, source_target_pairs={{0,2},{1,3},{2,0},{3,1},{4,6},{5,7},{6,4},{7,5},{8,10},{9,11},{10,... | collective-permute-start | bytes 276488 | tf_op jit(solution)/shard_map/ppermute | solution.py:15
  22.3 2.8 %collective-permute-done.3 = bf16[45,1024]{1,0:T(8,128)(2,1)S(1)} collective-permute-done((bf16[45,1024]{1,0:T(8,128)(2,1)S(1)}, bf16[45,1024]{1,0:T(8,128)(2,1)S(1)}, u32[]{:S(2)}, u32[]{:S(2)}) %collective-permute-start.3) | collective-permute-done | bytes 92192 | tf_op jit(solution)/shard_map/ppermute | solution.py:15
  25.2 0.1 collective-permute-start.4
  25.3 1.4 %collective-permute-done.4 = bf16[45,2048]{1,0:T(8,128)(2,1)S(1)} collective-permute-done((bf16[45,2048]{1,0:T(8,128)(2,1)S(1)}, bf16[45,2048]{1,0:T(8,128)(2,1)S(1)}, u32[]{:S(2)}, u32[]{:S(2)}) %collective-permute-start.4) | collective-permute-done | bytes 184352 | tf_op jit(solution)/shard_map/ppermute | solution.py:15
  26.7 0.1 broadcast_select_fusion.1
  26.8 0.8 %pad_maximum_fusion = bf16[45,4096]{1,0:T(8,128)(2,1)} fusion(bf16[45,1024]{1,0:T(8,128)(2,1)S(1)} %get-tuple-element.13, bf16[45,1024]{1,0:T(8,128)(2,1)S(1)} %get-tuple-element.8, bf16[45,1024]{1,0:T(8,128)(2,1)S(1)} %get-tuple-element.14, bf16[45,1024]{1,0:T(8,128)(2,1)S(1)} %get-tuple-element.7), kind=kLoop, calls=%fused_computation.4 | loop fusion | flops 1474560 | bytes 737280 | tf_op jit(solution)/shard_map/concatenate | solution.py:41
  (8 shorter events, 0.1 us)
Async XLA Ops:
  0.0 19.9 %copy-start = (s32[512]{0:T(512)S(1)}, s32[512]{0:T(512)}, u32[]{:S(2)}) copy-start(s32[512]{0:T(512)} %param.11) | copy-start | bytes 6148
  3.8 5.8 %collective-permute-start = (f32[184,128]{1,0:T(8,128)S(1)}, f32[184,128]{1,0:T(8,128)S(1)}, u32[]{:S(2)}, u32[]{:S(2)}) collective-permute-start(f32[184,128]{1,0:T(8,128)S(1)} %local_sums.1), channel_id=1, source_target_pairs={{0,4},{4,0},{8,12},{12,8},{16,20},{20,16},{24,28},{28,24},{1,5},{5... | collective-permute-start | bytes 282632 | tf_op jit(solution)/shard_map/ppermute | solution.py:15
  9.6 4.6 %collective-permute-start.1 = (f32[184,128]{1,0:T(8,128)S(1)}, f32[184,128]{1,0:T(8,128)S(1)}, u32[]{:S(2)}, u32[]{:S(2)}) collective-permute-start(f32[184,128]{1,0:T(8,128)S(1)} %add.9), channel_id=1, source_target_pairs={{0,8},{4,12},{8,0},{12,4},{16,24},{20,28},{24,16},{28,20},{1,9},{5... | collective-permute-start | bytes 282632 | tf_op jit(solution)/shard_map/ppermute | solution.py:15
  14.3 5.6 %collective-permute-start.2 = (f32[184,128]{1,0:T(8,128)S(1)}, f32[184,128]{1,0:T(8,128)S(1)}, u32[]{:S(2)}, u32[]{:S(2)}) collective-permute-start(f32[184,128]{1,0:T(8,128)S(1)} %add.10), channel_id=1, source_target_pairs={{0,16},{4,20},{8,24},{12,28},{16,0},{20,4},{24,8},{28,12},{1,17},{... | collective-permute-start | bytes 282632 | tf_op jit(solution)/shard_map/ppermute | solution.py:15
  20.4 4.7 %collective-permute-start.3 = (bf16[45,1024]{1,0:T(8,128)(2,1)S(1)}, bf16[45,1024]{1,0:T(8,128)(2,1)S(1)}, u32[]{:S(2)}, u32[]{:S(2)}) collective-permute-start(bf16[45,1024]{1,0:T(8,128)(2,1)S(1)} %fusion.1), channel_id=1, source_target_pairs={{0,2},{1,3},{2,0},{3,1},{4,6},{5,7},{6,4},{7,5},{8,10},{9,11},{10,... | collective-permute-start | bytes 276488 | tf_op jit(solution)/shard_map/ppermute | solution.py:15
  25.2 1.5 %collective-permute-start.4 = (bf16[45,2048]{1,0:T(8,128)(2,1)S(1)}, bf16[45,2048]{1,0:T(8,128)(2,1)S(1)}, u32[]{:S(2)}, u32[]{:S(2)}) collective-permute-start(bf16[45,2048]{1,0:T(8,128)(2,1)S(1)} %pad_maximum_fusion.1), channel_id=1, source_target_pairs={{0,1},{1,0},{2,3},{3,2},{4,5},{5,4},{6,7},{7,6},{8,9},{9,8},{10,11... | collective-permute-start | bytes 552968 | tf_op jit(solution)/shard_map/ppermute | solution.py:15

commit v4 on v3

--- a/solution.py
+++ b/solution.py
@@ -9,38 +9,11 @@
 
 GRID_DEV = 1024
 LANES = 128
+SPLIT = 32
 
 
 def exchange(value, axis, size, bit):
     return lax.ppermute(value, axis, [(i, i ^ bit) for i in range(size)])
-
-
-def butterfly_sum(value, axis, size):
-    if size & (size - 1):
-        return lax.psum(value, axis)
-    bit = 1
-    while bit < size:
-        value = value + exchange(value, axis, size, bit)
-        bit *= 2
-    return value
-
-
-def butterfly_gather(value, axis, size):
-    if size & (size - 1):
-        return lax.all_gather(value, axis, axis=1, tiled=True)
-    index = lax.axis_index(axis)
-    width = value.shape[1]
-    bit = size // 2
-    while bit:
-        other = exchange(value, axis, size, bit)
-        low = (index & bit) == 0
-        first, second = jnp.where(low, value, other), jnp.where(low, other, value)
-        blocks = []
-        for start in range(0, value.shape[1], width):
-            blocks += [first[:, start : start + width], second[:, start : start + width]]
-        value = jnp.concatenate(blocks, axis=1)
-        bit //= 2
-    return value
 
 
 def sums_kernel(
@@ -138,14 +111,90 @@
     )(*[pltpu.with_memory_space_constraint(x, pltpu.HBM) for x in (turned, fod, modulation, subject_ids, subject_weight)])
 
 
+def finish_kernel(coef, mine_ref, other_ref, cells_ref, out_ref, total):
+    rows, voxels = out_ref.shape
+    blocks = voxels // LANES
+    total[pl.ds(0, mine_ref.shape[0])] = mine_ref[...] + other_ref[...]
+    row = lax.broadcasted_iota(jnp.int32, (rows, LANES), 0)
+    for block in range(blocks):
+        numer = total[pl.ds(block, rows, stride=blocks)]
+        denom = total[pl.ds(coef * blocks + block, 1)]
+        cells = cells_ref[pl.ds(block, 1)]
+        high, low = (cells // SPLIT).astype(jnp.float32), (cells % SPLIT).astype(jnp.float32)
+        value = jnp.where(row < coef, numer / denom, jnp.where(row == coef, high, jnp.where(row == coef + 1, low, 0.0)))
+        out_ref[:, pl.ds(block * LANES, LANES)] = value.astype(jnp.bfloat16)
+
+
+def finish(mine, other, cells, coef):
+    blocks = cells.shape[0] // LANES
+    rows = -(-(coef + 2) // 8) * 8
+    return pl.pallas_call(
+        functools.partial(finish_kernel, coef),
+        out_shape=pltpu.VMEM((rows, cells.shape[0]), jnp.bfloat16),
+        in_specs=[pl.BlockSpec(memory_space=pltpu.VMEM)] * 3,
+        out_specs=pl.BlockSpec(memory_space=pltpu.VMEM),
+        scratch_shapes=[pltpu.VMEM((rows * blocks, LANES), jnp.float32)],
+        compiler_params=pltpu.CompilerParams(vmem_limit_bytes=16 << 20),
+        name="finish",
+    )(mine, other, cells.reshape(blocks, LANES))
+
+
+def dense_of(coef, compact):
+    voxels = compact.shape[1]
+    high = compact[coef : coef + 1].astype(jnp.float32)
+    low = compact[coef + 1 : coef + 2].astype(jnp.float32)
+    cells = (high * SPLIT + low).astype(jnp.int32)
+    hit = lax.broadcasted_iota(jnp.int32, (GRID_DEV, voxels), 0) == cells
+    onehot = jnp.where(hit, 1.0, 0.0).astype(jnp.bfloat16)
+    dense = lax.dot_general(compact, onehot, (((1,), (1,)), ((), ())), preferred_element_type=jnp.float32)
+    return dense[:coef].astype(jnp.bfloat16)
+
+
+def place_first_kernel(coef, compact_ref, out_ref):
+    out_ref[...] = dense_of(coef, compact_ref[...])
+
+
+def place_next_kernel(coef, first_ref, compact_ref, out_ref):
+    width = first_ref.shape[1]
+    out_ref[:, pl.ds(0, width)] = first_ref[...]
+    out_ref[:, pl.ds(width, GRID_DEV)] = dense_of(coef, compact_ref[...])
+
+
+def place(coef, first, compact):
+    operands = (compact,) if first is None else (first, compact)
+    width = GRID_DEV if first is None else first.shape[1] + GRID_DEV
+    return pl.pallas_call(
+        functools.partial(place_first_kernel if first is None else place_next_kernel, coef),
+        out_shape=pltpu.VMEM((coef, width), jnp.bfloat16),
+        in_specs=[pl.BlockSpec(memory_space=pltpu.VMEM)] * len(operands),
+        out_specs=pl.BlockSpec(memory_space=pltpu.VMEM),
+        cost_estimate=pl.CostEstimate(flops=2 * coef * compact.shape[1] * GRID_DEV, bytes_accessed=1 << 18, transcendentals=0),
+        compiler_params=pltpu.CompilerParams(vmem_limit_bytes=32 << 20),
+        name="place",
+    )(*operands)
+
+
 def on_device(subj, slab, fod, rotation, modulation, subject_ids, subject_weight, voxel_cell_index):
-    coef, voxels = fod.shape[1:]
-    sums = local_sums(fod, rotation, modulation, subject_ids, subject_weight)
-    sums = butterfly_sum(sums, "subj", subj).reshape(coef + 1, voxels)
-    average = (sums[:coef] / sums[coef:]).astype(jnp.bfloat16)
-    onehot = (voxel_cell_index[:, None] == jnp.arange(GRID_DEV, dtype=jnp.int32)[None, :]).astype(jnp.bfloat16)
-    dense = jnp.dot(average, onehot, preferred_element_type=jnp.float32).astype(jnp.bfloat16)
-    return butterfly_gather(dense, "slab", slab)
+    coef = fod.shape[1]
+    mine = local_sums(fod, rotation, modulation, subject_ids, subject_weight)
+    bit = 1
+    while 2 * bit < subj:
+        mine = mine + exchange(mine, "subj", subj, bit)
+        bit *= 2
+    compact = finish(mine, exchange(mine, "subj", subj, bit), voxel_cell_index, coef)
+    bits = [1 << n for n in reversed(range(slab.bit_length() - 1))]
+    other = exchange(compact, "slab", slab, bits[0])
+    dense = place(coef, place(coef, None, compact), other)
+    order = [0, bits[0]]
+    for bit in bits[1:]:
+        dense = jnp.concatenate([dense, exchange(dense, "slab", slab, bit)], axis=1)
+        order += [o ^ bit for o in order]
+    index = lax.axis_index("slab")
+    blocks = {o: dense[:, i * GRID_DEV : (i + 1) * GRID_DEV] for i, o in enumerate(order)}
+    for bit in bits:
+        flip = (index & bit) != 0
+        blocks = {o: jnp.where(flip, blocks[o ^ bit], blocks[o]) for o in blocks}
+    return jnp.concatenate([blocks[o] for o in range(slab)], axis=1)
 
 
 def solution(mesh):

time: 27.8 us -> 27 us (0.971)
  waiting for transfers between devices: 12.1 us -> 11.1 us
  Pallas kernels: 3.81 us -> 4.76 us
  matrix products: 0.57 us -> 0 us
    ppermute x5, waiting for transfers between devices: 12.1 us -> 11.1 us  [exchange(): return lax.ppermute(value, axis, [(i, i ^ bit) for i in range(size)])]
    pallas_call x0 -> x3, Pallas kernels: none -> 0.95 us  [the longest x2 0.91 us: place(): pl.pallas_call(functools.partial(place_first_kernel if first is None else...]
    dot_general x1 -> x0, matrix products: 0.57 us -> none  [on_device(): jnp.dot(average, onehot, preferred_element_type=jnp.float32)]
    concatenate x2 -> x1, other arithmetic: 0.79 us -> 0.77 us  [on_device(): return jnp.concatenate([blocks[o] for o in range(slab)], axis=1)]
  transfers between devices with their start and end apart: 5 -> 5, of which waited for: 5 -> 5; matrix products, arithmetic and copies ran while one was open for 0% -> 0% of each run, Pallas kernels for 0% -> 2%
where the time goes in v4:
time: 27 us; the launch traced here: 26.8 us
  waiting for transfers between devices  11.1 us (41%)
  starting transfers between devices  10 us (37%)
  Pallas kernels  4.76 us (18%)
  other arithmetic  0.83 us (3%)
    ppermute x5, waiting for transfers between devices, exchange(): return lax.ppermute(value, axis, [(i, i ^ bit) for i in range(size)])  11.1 us
    ppermute x5, starting transfers between devices, exchange(): return lax.ppermute(value, axis, [(i, i ^ bit) for i in range(size)])  10 us
    pallas_call x1, Pallas kernels, local_sums(): pl.pallas_call(functools.partial(sums_kernel, subjects, chunk), out_shape...  3.81 us
    pallas_call x2, Pallas kernels, place(): pl.pallas_call(functools.partial(place_first_kernel if first is None else...  0.91 us
    concatenate x1, other arithmetic, on_device(): return jnp.concatenate([blocks[o] for o in range(slab)], axis=1)  0.77 us
  transfers between devices with their start and end apart: 5, of which 5 were waited for; matrix products, arithmetic and copies ran while one was open for 0% of the time, Pallas kernels for 2%

profile of v4, /device:TPU:0, one launch (start us, length us, event | category | flops | bytes accessed | tf_op | source)
XLA Modules:
  0.0 26.8 jit_solution(14890360667998307966)
XLA Ops:
  0.0 0.0 copy-start
  0.0 3.8 %local_sums.1 = f32[184,128]{1,0:T(8,128)S(1)} custom-call(bf16[45,45,16,128]{3,2,1,0:T(8,128)(2,1)} %bitcast.21, bf16[45,16,128]{2,1,0:T(8,128)(2,1)} %bitcast.22, f32[16,128]{1,0:T(8,128)} %bitcast.23, s32[4]{0:T(128)} %ids_hbm.1, f32[32]{0:T(128)} %study_hbm.1), custom_call_target="tpu_custom_call" | custom-call | tf_op jit(solution)/shard_map/local_sums/pallas_call | solution.py:93
  3.8 3.1 %collective-permute-start = (f32[184,128]{1,0:T(8,128)S(1)}, f32[184,128]{1,0:T(8,128)S(1)}, u32[]{:S(2)}, u32[]{:S(2)}) collective-permute-start(f32[184,128]{1,0:T(8,128)S(1)} %local_sums.1), channel_id=1, source_target_pairs={{0,4},{4,0},{8,12},{12,8},{16,20},{20,16},{24,28},{28,24},{1,5},{5... | collective-permute-start | bytes 282632 | tf_op jit(solution)/shard_map/ppermute | solution.py:16
  6.9 2.7 %collective-permute-done = f32[184,128]{1,0:T(8,128)S(1)} collective-permute-done((f32[184,128]{1,0:T(8,128)S(1)}, f32[184,128]{1,0:T(8,128)S(1)}, u32[]{:S(2)}, u32[]{:S(2)}) %collective-permute-start) | collective-permute-done | bytes 94240 | tf_op jit(solution)/shard_map/ppermute | solution.py:16
  9.6 2.0 %collective-permute-start.1 = (f32[184,128]{1,0:T(8,128)S(1)}, f32[184,128]{1,0:T(8,128)S(1)}, u32[]{:S(2)}, u32[]{:S(2)}) collective-permute-start(f32[184,128]{1,0:T(8,128)S(1)} %add.6), channel_id=1, source_target_pairs={{0,8},{4,12},{8,0},{12,4},{16,24},{20,28},{24,16},{28,20},{1,9},{5... | collective-permute-start | bytes 282632 | tf_op jit(solution)/shard_map/ppermute | solution.py:16
  11.6 2.6 %collective-permute-done.1 = f32[184,128]{1,0:T(8,128)S(1)} collective-permute-done((f32[184,128]{1,0:T(8,128)S(1)}, f32[184,128]{1,0:T(8,128)S(1)}, u32[]{:S(2)}, u32[]{:S(2)}) %collective-permute-start.1) | collective-permute-done | bytes 94240 | tf_op jit(solution)/shard_map/ppermute | solution.py:16
  14.3 3.0 %collective-permute-start.2 = (f32[184,128]{1,0:T(8,128)S(1)}, f32[184,128]{1,0:T(8,128)S(1)}, u32[]{:S(2)}, u32[]{:S(2)}) collective-permute-start(f32[184,128]{1,0:T(8,128)S(1)} %add.7.mine_ref), channel_id=1, source_target_pairs={{0,16},{4,20},{8,24},{12,28},{16,0},{20,4},{24,8},{28,12},{1,17},{... | collective-permute-start | bytes 282632 | tf_op jit(solution)/shard_map/ppermute | solution.py:16
  17.3 2.6 %collective-permute-done.2.other_ref = f32[184,128]{1,0:T(8,128)S(1)} collective-permute-done((f32[184,128]{1,0:T(8,128)S(1)}, f32[184,128]{1,0:T(8,128)S(1)}, u32[]{:S(2)}, u32[]{:S(2)}) %collective-permute-start.2) | collective-permute-done | bytes 94240 | tf_op jit(solution)/shard_map/ppermute | solution.py:16
  19.8 0.0 copy-done
  19.9 1.9 %collective-permute-start.3 = (bf16[48,512]{1,0:T(8,128)(2,1)S(1)}, bf16[48,512]{1,0:T(8,128)(2,1)S(1)}, u32[]{:S(2)}, u32[]{:S(2)}) collective-permute-start(bf16[48,512]{1,0:T(8,128)(2,1)S(1)} %finish.1.compact_ref), channel_id=1, source_target_pairs={{0,2},{1,3},{2,0},{3,1},{4,6},{5,7},{6,4},{7,5},{8,10},{9,11},{10,... | collective-permute-start | bytes 147464 | tf_op jit(solution)/shard_map/ppermute | solution.py:16
  21.7 0.5 %place.2.first_ref = bf16[45,1024]{1,0:T(8,128)(2,1)S(1)} custom-call(bf16[48,512]{1,0:T(8,128)(2,1)S(1)} %finish.1.compact_ref), custom_call_target="tpu_custom_call" | custom-call | flops 47185920 | bytes 262144 | tf_op jit(solution)/shard_map/place/pallas_call | solution.py:166
  22.2 1.8 %collective-permute-done.3.compact_ref = bf16[48,512]{1,0:T(8,128)(2,1)S(1)} collective-permute-done((bf16[48,512]{1,0:T(8,128)(2,1)S(1)}, bf16[48,512]{1,0:T(8,128)(2,1)S(1)}, u32[]{:S(2)}, u32[]{:S(2)}) %collective-permute-start.3) | collective-permute-done | bytes 49184 | tf_op jit(solution)/shard_map/ppermute | solution.py:16
  24.0 0.5 %place.3 = bf16[45,2048]{1,0:T(8,128)(2,1)S(1)} custom-call(bf16[45,1024]{1,0:T(8,128)(2,1)S(1)} %place.2.first_ref, bf16[48,512]{1,0:T(8,128)(2,1)S(1)} %collective-permute-done.3.compact_ref), custom_call_target="tpu_custom_call" | custom-call | flops 47185920 | bytes 262144 | tf_op jit(solution)/shard_map/place/pallas_call | solution.py:166
  24.5 0.1 collective-permute-start.4
  24.6 1.4 %collective-permute-done.4 = bf16[45,2048]{1,0:T(8,128)(2,1)S(1)} collective-permute-done((bf16[45,2048]{1,0:T(8,128)(2,1)S(1)}, bf16[45,2048]{1,0:T(8,128)(2,1)S(1)}, u32[]{:S(2)}, u32[]{:S(2)}) %collective-permute-start.4) | collective-permute-done | bytes 184352 | tf_op jit(solution)/shard_map/ppermute | solution.py:16
  26.0 0.8 %pad_maximum_fusion = bf16[45,4096]{1,0:T(8,128)(2,1)} fusion(bf16[45,1024]{1,0:T(8,128)(2,1)S(1)} %get-tuple-element.8, bf16[45,1024]{1,0:T(8,128)(2,1)S(1)} %get-tuple-element.7, bf16[45,1024]{1,0:T(8,128)(2,1)S(1)} %get-tuple-element.6, bf16[45,1024]{1,0:T(8,128)(2,1)S(1)} %get-tuple-element.5), kind=kLoop, calls=%fused_computation | loop fusion | flops 1474560 | bytes 737280 | tf_op jit(solution)/shard_map/concatenate | solution.py:197
  (4 shorter events, 0.1 us)
Async XLA Ops:
  0.0 19.8 %copy-start = (s32[512]{0:T(512)S(1)}, s32[512]{0:T(512)}, u32[]{:S(2)}) copy-start(s32[512]{0:T(512)} %param.11) | copy-start | bytes 6148
  3.8 5.8 %collective-permute-start = (f32[184,128]{1,0:T(8,128)S(1)}, f32[184,128]{1,0:T(8,128)S(1)}, u32[]{:S(2)}, u32[]{:S(2)}) collective-permute-start(f32[184,128]{1,0:T(8,128)S(1)} %local_sums.1), channel_id=1, source_target_pairs={{0,4},{4,0},{8,12},{12,8},{16,20},{20,16},{24,28},{28,24},{1,5},{5... | collective-permute-start | bytes 282632 | tf_op jit(solution)/shard_map/ppermute | solution.py:16
  9.6 4.6 %collective-permute-start.1 = (f32[184,128]{1,0:T(8,128)S(1)}, f32[184,128]{1,0:T(8,128)S(1)}, u32[]{:S(2)}, u32[]{:S(2)}) collective-permute-start(f32[184,128]{1,0:T(8,128)S(1)} %add.6), channel_id=1, source_target_pairs={{0,8},{4,12},{8,0},{12,4},{16,24},{20,28},{24,16},{28,20},{1,9},{5... | collective-permute-start | bytes 282632 | tf_op jit(solution)/shard_map/ppermute | solution.py:16
  14.3 5.6 %collective-permute-start.2 = (f32[184,128]{1,0:T(8,128)S(1)}, f32[184,128]{1,0:T(8,128)S(1)}, u32[]{:S(2)}, u32[]{:S(2)}) collective-permute-start(f32[184,128]{1,0:T(8,128)S(1)} %add.7.mine_ref), channel_id=1, source_target_pairs={{0,16},{4,20},{8,24},{12,28},{16,0},{20,4},{24,8},{28,12},{1,17},{... | collective-permute-start | bytes 282632 | tf_op jit(solution)/shard_map/ppermute | solution.py:16
  19.9 4.2 %collective-permute-start.3 = (bf16[48,512]{1,0:T(8,128)(2,1)S(1)}, bf16[48,512]{1,0:T(8,128)(2,1)S(1)}, u32[]{:S(2)}, u32[]{:S(2)}) collective-permute-start(bf16[48,512]{1,0:T(8,128)(2,1)S(1)} %finish.1.compact_ref), channel_id=1, source_target_pairs={{0,2},{1,3},{2,0},{3,1},{4,6},{5,7},{6,4},{7,5},{8,10},{9,11},{10,... | collective-permute-start | bytes 147464 | tf_op jit(solution)/shard_map/ppermute | solution.py:16
  24.5 1.5 %collective-permute-start.4 = (bf16[45,2048]{1,0:T(8,128)(2,1)S(1)}, bf16[45,2048]{1,0:T(8,128)(2,1)S(1)}, u32[]{:S(2)}, u32[]{:S(2)}) collective-permute-start(bf16[45,2048]{1,0:T(8,128)(2,1)S(1)} %place.3), channel_id=1, source_target_pairs={{0,1},{1,0},{2,3},{3,2},{4,5},{5,4},{6,7},{7,6},{8,9},{9,8},{10,11... | collective-permute-start | bytes 552968 | tf_op jit(solution)/shard_map/ppermute | solution.py:16

commit v5 on v4

--- a/solution.py
+++ b/solution.py
@@ -10,6 +10,7 @@
 GRID_DEV = 1024
 LANES = 128
 SPLIT = 32
+TILE = 256
 
 
 def exchange(value, axis, size, bit):
@@ -144,34 +145,62 @@
     high = compact[coef : coef + 1].astype(jnp.float32)
     low = compact[coef + 1 : coef + 2].astype(jnp.float32)
     cells = (high * SPLIT + low).astype(jnp.int32)
-    hit = lax.broadcasted_iota(jnp.int32, (GRID_DEV, voxels), 0) == cells
-    onehot = jnp.where(hit, 1.0, 0.0).astype(jnp.bfloat16)
-    dense = lax.dot_general(compact, onehot, (((1,), (1,)), ((), ())), preferred_element_type=jnp.float32)
-    return dense[:coef].astype(jnp.bfloat16)
-
-
-def place_first_kernel(coef, compact_ref, out_ref):
+    tiles = []
+    for start in range(0, GRID_DEV, TILE):
+        first = max(start - (GRID_DEV - voxels), 0) // TILE * TILE
+        last = min(start + TILE, voxels)
+        hit = lax.broadcasted_iota(jnp.int32, (TILE, last - first), 0) + start == cells[:, first:last]
+        onehot = jnp.where(hit, 1.0, 0.0).astype(jnp.bfloat16)
+        tiles.append(
+            lax.dot_general(compact[:, first:last], onehot, (((1,), (1,)), ((), ())), preferred_element_type=jnp.float32)
+        )
+    return jnp.concatenate(tiles, axis=1)[:coef].astype(jnp.bfloat16)
+
+
+def place_kernel(coef, compact_ref, out_ref):
     out_ref[...] = dense_of(coef, compact_ref[...])
 
 
-def place_next_kernel(coef, first_ref, compact_ref, out_ref):
-    width = first_ref.shape[1]
-    out_ref[:, pl.ds(0, width)] = first_ref[...]
-    out_ref[:, pl.ds(width, GRID_DEV)] = dense_of(coef, compact_ref[...])
-
-
-def place(coef, first, compact):
-    operands = (compact,) if first is None else (first, compact)
-    width = GRID_DEV if first is None else first.shape[1] + GRID_DEV
-    return pl.pallas_call(
-        functools.partial(place_first_kernel if first is None else place_next_kernel, coef),
-        out_shape=pltpu.VMEM((coef, width), jnp.bfloat16),
-        in_specs=[pl.BlockSpec(memory_space=pltpu.VMEM)] * len(operands),
+def place(coef, compact):
+    return pl.pallas_call(
+        functools.partial(place_kernel, coef),
+        out_shape=pltpu.VMEM((coef, GRID_DEV), jnp.bfloat16),
+        in_specs=[pl.BlockSpec(memory_space=pltpu.VMEM)],
         out_specs=pl.BlockSpec(memory_space=pltpu.VMEM),
         cost_estimate=pl.CostEstimate(flops=2 * coef * compact.shape[1] * GRID_DEV, bytes_accessed=1 << 18, transcendentals=0),
         compiler_params=pltpu.CompilerParams(vmem_limit_bytes=32 << 20),
         name="place",
-    )(*operands)
+    )(compact)
+
+
+def template_kernel(coef, order, *refs):
+    *ready, compact_ref, out_ref, last, sem = refs
+    index = lax.axis_index("slab")
+
+    def write(i, ref):
+        columns = pl.ds(pl.multiple_of((index ^ order[i]) * GRID_DEV, GRID_DEV), GRID_DEV)
+        return pltpu.make_async_copy(ref, out_ref.at[:, columns], sem.at[i])
+
+    copies = [write(i, ref) for i, ref in enumerate(ready)]
+    for copy in copies:
+        copy.start()
+    last[...] = dense_of(coef, compact_ref[...])
+    copies.append(write(len(ready), last))
+    copies[-1].start()
+    for copy in copies:
+        copy.wait()
+
+
+def template(coef, order, ready, compact):
+    return pl.pallas_call(
+        functools.partial(template_kernel, coef, order),
+        out_shape=jax.ShapeDtypeStruct((coef, len(order) * GRID_DEV), jnp.bfloat16),
+        in_specs=[pl.BlockSpec(memory_space=pltpu.VMEM)] * len(order),
+        out_specs=pl.BlockSpec(memory_space=pl.ANY),
+        scratch_shapes=[pltpu.VMEM((coef, GRID_DEV), jnp.bfloat16), pltpu.SemaphoreType.DMA((len(order),))],
+        compiler_params=pltpu.CompilerParams(vmem_limit_bytes=32 << 20),
+        name="template",
+    )(*ready, compact)
 
 
 def on_device(subj, slab, fod, rotation, modulation, subject_ids, subject_weight, voxel_cell_index):
@@ -181,20 +210,21 @@
     while 2 * bit < subj:
         mine = mine + exchange(mine, "subj", subj, bit)
         bit *= 2
-    compact = finish(mine, exchange(mine, "subj", subj, bit), voxel_cell_index, coef)
-    bits = [1 << n for n in reversed(range(slab.bit_length() - 1))]
-    other = exchange(compact, "slab", slab, bits[0])
-    dense = place(coef, place(coef, None, compact), other)
-    order = [0, bits[0]]
-    for bit in bits[1:]:
-        dense = jnp.concatenate([dense, exchange(dense, "slab", slab, bit)], axis=1)
-        order += [o ^ bit for o in order]
-    index = lax.axis_index("slab")
-    blocks = {o: dense[:, i * GRID_DEV : (i + 1) * GRID_DEV] for i, o in enumerate(order)}
-    for bit in bits:
-        flip = (index & bit) != 0
-        blocks = {o: jnp.where(flip, blocks[o ^ bit], blocks[o]) for o in blocks}
-    return jnp.concatenate([blocks[o] for o in range(slab)], axis=1)
+    pieces = {0: finish(mine, exchange(mine, "subj", subj, bit), voxel_cell_index, coef)}
+    pieces[1] = exchange(pieces[0], "slab", slab, 1)
+    dense = {o: place(coef, piece) for o, piece in pieces.items()}
+    bit = slab // 2
+    while bit > 1:
+        for o in [o for o in pieces if not o & 1]:
+            far = o ^ bit
+            pieces[far] = exchange(pieces[o], "slab", slab, bit)
+            dense, pieces[far] = lax.optimization_barrier((dense, pieces[far]))
+            pieces[far ^ 1] = exchange(pieces[far], "slab", slab, 1)
+            dense[far] = place(coef, pieces[far])
+            if len(pieces) < slab:
+                dense[far ^ 1] = place(coef, pieces[far ^ 1])
+        bit //= 2
+    return template(coef, (*dense, last := list(pieces)[-1]), list(dense.values()), pieces[last])
 
 
 def solution(mesh):

time: 27 us -> 26.6 us (0.985)
  Pallas kernels: 4.76 us -> 5.94 us
  other arithmetic: 0.83 us -> 0.02 us
  waiting for transfers between devices: 11.1 us -> 10.4 us
    pallas_call x2 -> x4, Pallas kernels: 0.91 us -> 2.1 us  [the longest x3 1.06 us: place(): pl.pallas_call(functools.partial(place_kernel, coef), out_shape=pltpu.VME...]
    concatenate x1 -> x0, other arithmetic: 0.77 us -> none  [on_device(): return jnp.concatenate([blocks[o] for o in range(slab)], axis=1)]
    ppermute x5 -> x6, waiting for transfers between devices: 11.1 us -> 10.4 us  [exchange(): return lax.ppermute(value, axis, [(i, i ^ bit) for i in range(size)])]
    ppermute x5 -> x6, starting transfers between devices: 10 us -> 10 us  [exchange(): return lax.ppermute(value, axis, [(i, i ^ bit) for i in range(size)])]
  transfers between devices with their start and end apart: 5 -> 6, of which waited for: 5 -> 5; matrix products, arithmetic and copies ran while one was open for 0% -> 0% of each run, Pallas kernels for 2% -> 4%
where the time goes in v5:
time: 26.6 us; the launch traced here: 26.4 us
  waiting for transfers between devices  10.4 us (39%)
  starting transfers between devices  10 us (38%)
  Pallas kernels  5.94 us (22%)
    ppermute x6, waiting for transfers between devices, exchange(): return lax.ppermute(value, axis, [(i, i ^ bit) for i in range(size)])  10.4 us
    ppermute x6, starting transfers between devices, exchange(): return lax.ppermute(value, axis, [(i, i ^ bit) for i in range(size)])  10 us
    pallas_call x1, Pallas kernels, local_sums(): pl.pallas_call(functools.partial(sums_kernel, subjects, chunk), out_shape...  3.81 us
    pallas_call x3, Pallas kernels, place(): pl.pallas_call(functools.partial(place_kernel, coef), out_shape=pltpu.VME...  1.06 us
    pallas_call x1, Pallas kernels, template(): pl.pallas_call(functools.partial(template_kernel, coef, order), out_shape...  1.03 us
  transfers between devices with their start and end apart: 6, of which 5 were waited for; matrix products, arithmetic and copies ran while one was open for 0% of the time, Pallas kernels for 4%

profile of v5, /device:TPU:0, one launch (start us, length us, event | category | flops | bytes accessed | tf_op | source)
XLA Modules:
  0.0 26.4 jit_solution(545873142991124495)
XLA Ops:
  0.0 0.0 copy-start
  0.0 3.8 %local_sums.1 = f32[184,128]{1,0:T(8,128)S(1)} custom-call(bf16[45,45,16,128]{3,2,1,0:T(8,128)(2,1)} %bitcast.21, bf16[45,16,128]{2,1,0:T(8,128)(2,1)} %bitcast.22, f32[16,128]{1,0:T(8,128)} %bitcast.23, s32[4]{0:T(128)} %ids_hbm.1, f32[32]{0:T(128)} %study_hbm.1), custom_call_target="tpu_custom_call" | custom-call | tf_op jit(solution)/shard_map/local_sums/pallas_call | solution.py:94
  3.8 3.1 %collective-permute-start = (f32[184,128]{1,0:T(8,128)S(1)}, f32[184,128]{1,0:T(8,128)S(1)}, u32[]{:S(2)}, u32[]{:S(2)}) collective-permute-start(f32[184,128]{1,0:T(8,128)S(1)} %local_sums.1), channel_id=1, source_target_pairs={{0,4},{4,0},{8,12},{12,8},{16,20},{20,16},{24,28},{28,24},{1,5},{5... | collective-permute-start | bytes 282632 | tf_op jit(solution)/shard_map/ppermute | solution.py:17
  6.9 2.7 %collective-permute-done = f32[184,128]{1,0:T(8,128)S(1)} collective-permute-done((f32[184,128]{1,0:T(8,128)S(1)}, f32[184,128]{1,0:T(8,128)S(1)}, u32[]{:S(2)}, u32[]{:S(2)}) %collective-permute-start) | collective-permute-done | bytes 94240 | tf_op jit(solution)/shard_map/ppermute | solution.py:17
  9.6 2.0 %collective-permute-start.1 = (f32[184,128]{1,0:T(8,128)S(1)}, f32[184,128]{1,0:T(8,128)S(1)}, u32[]{:S(2)}, u32[]{:S(2)}) collective-permute-start(f32[184,128]{1,0:T(8,128)S(1)} %add.6), channel_id=1, source_target_pairs={{0,8},{4,12},{8,0},{12,4},{16,24},{20,28},{24,16},{28,20},{1,9},{5... | collective-permute-start | bytes 282632 | tf_op jit(solution)/shard_map/ppermute | solution.py:17
  11.6 2.6 %collective-permute-done.1 = f32[184,128]{1,0:T(8,128)S(1)} collective-permute-done((f32[184,128]{1,0:T(8,128)S(1)}, f32[184,128]{1,0:T(8,128)S(1)}, u32[]{:S(2)}, u32[]{:S(2)}) %collective-permute-start.1) | collective-permute-done | bytes 94240 | tf_op jit(solution)/shard_map/ppermute | solution.py:17
  14.3 3.0 %collective-permute-start.2 = (f32[184,128]{1,0:T(8,128)S(1)}, f32[184,128]{1,0:T(8,128)S(1)}, u32[]{:S(2)}, u32[]{:S(2)}) collective-permute-start(f32[184,128]{1,0:T(8,128)S(1)} %add.7.mine_ref), channel_id=1, source_target_pairs={{0,16},{4,20},{8,24},{12,28},{16,0},{20,4},{24,8},{28,12},{1,17},{... | collective-permute-start | bytes 282632 | tf_op jit(solution)/shard_map/ppermute | solution.py:17
  17.3 2.6 %collective-permute-done.2.other_ref = f32[184,128]{1,0:T(8,128)S(1)} collective-permute-done((f32[184,128]{1,0:T(8,128)S(1)}, f32[184,128]{1,0:T(8,128)S(1)}, u32[]{:S(2)}, u32[]{:S(2)}) %collective-permute-start.2) | collective-permute-done | bytes 94240 | tf_op jit(solution)/shard_map/ppermute | solution.py:17
  19.8 0.0 copy-done
  19.9 0.1 collective-permute-start.3
  19.9 1.9 %collective-permute-start.4 = (bf16[48,512]{1,0:T(8,128)(2,1)S(1)}, bf16[48,512]{1,0:T(8,128)(2,1)S(1)}, u32[]{:S(2)}, u32[]{:S(2)}) collective-permute-start(bf16[48,512]{1,0:T(8,128)(2,1)S(1)} %finish.1.compact_ref), channel_id=1, source_target_pairs={{0,2},{1,3},{2,0},{3,1},{4,6},{5,7},{6,4},{7,5},{8,10},{9,11},{10,... | collective-permute-start | bytes 147464 | tf_op jit(solution)/shard_map/ppermute | solution.py:17
  21.8 0.4 %place.3.refs_0_ = bf16[45,1024]{1,0:T(8,128)(2,1)S(1)} custom-call(bf16[48,512]{1,0:T(8,128)(2,1)S(1)} %finish.1.compact_ref), custom_call_target="tpu_custom_call" | custom-call | flops 47185920 | bytes 262144 | tf_op jit(solution)/shard_map/place/pallas_call | solution.py:165
  22.2 0.0 collective-permute-done.3.compact_ref
  22.2 0.4 %place.4.refs_1_ = bf16[45,1024]{1,0:T(8,128)(2,1)S(1)} custom-call(bf16[48,512]{1,0:T(8,128)(2,1)S(1)} %collective-permute-done.3.compact_ref), custom_call_target="tpu_custom_call" | custom-call | flops 47185920 | bytes 262144 | tf_op jit(solution)/shard_map/place/pallas_call | solution.py:165
  22.6 1.6 %collective-permute-done.4.compact_ref = bf16[48,512]{1,0:T(8,128)(2,1)S(1)} collective-permute-done((bf16[48,512]{1,0:T(8,128)(2,1)S(1)}, bf16[48,512]{1,0:T(8,128)(2,1)S(1)}, u32[]{:S(2)}, u32[]{:S(2)}) %collective-permute-start.4) | collective-permute-done | bytes 49184 | tf_op jit(solution)/shard_map/ppermute | solution.py:17
  24.2 0.0 collective-permute-start.5
  24.2 0.4 %place.5.refs_2_ = bf16[45,1024]{1,0:T(8,128)(2,1)S(1)} custom-call(bf16[48,512]{1,0:T(8,128)(2,1)S(1)} %collective-permute-done.4.compact_ref), custom_call_target="tpu_custom_call" | custom-call | flops 47185920 | bytes 262144 | tf_op jit(solution)/shard_map/place/pallas_call | solution.py:165
  24.5 0.9 %collective-permute-done.5.refs_3_ = bf16[48,512]{1,0:T(8,128)(2,1)S(1)} collective-permute-done((bf16[48,512]{1,0:T(8,128)(2,1)S(1)}, bf16[48,512]{1,0:T(8,128)(2,1)S(1)}, u32[]{:S(2)}, u32[]{:S(2)}) %collective-permute-start.5) | collective-permute-done | bytes 49184 | tf_op jit(solution)/shard_map/ppermute | solution.py:17
  25.4 1.0 %template.1 = bf16[45,4096]{1,0:T(8,128)(2,1)} custom-call(bf16[45,1024]{1,0:T(8,128)(2,1)S(1)} %place.3.refs_0_, bf16[45,1024]{1,0:T(8,128)(2,1)S(1)} %place.4.refs_1_, bf16[45,1024]{1,0:T(8,128)(2,1)S(1)} %place.5.refs_2_, bf16[48,512]{1,0:T(8,128)(2,1)S(1)} %collective-permute-done.5.refs_3_), custom_call_target="tpu_custom_call" | custom-call | tf_op jit(solution)/shard_map/template/pallas_call | solution.py:195
  (3 shorter events, 0.1 us)
Async XLA Ops:
  0.0 19.8 %copy-start = (s32[512]{0:T(512)S(1)}, s32[512]{0:T(512)}, u32[]{:S(2)}) copy-start(s32[512]{0:T(512)} %param.11) | copy-start | bytes 6148
  3.8 5.8 %collective-permute-start = (f32[184,128]{1,0:T(8,128)S(1)}, f32[184,128]{1,0:T(8,128)S(1)}, u32[]{:S(2)}, u32[]{:S(2)}) collective-permute-start(f32[184,128]{1,0:T(8,128)S(1)} %local_sums.1), channel_id=1, source_target_pairs={{0,4},{4,0},{8,12},{12,8},{16,20},{20,16},{24,28},{28,24},{1,5},{5... | collective-permute-start | bytes 282632 | tf_op jit(solution)/shard_map/ppermute | solution.py:17
  9.6 4.6 %collective-permute-start.1 = (f32[184,128]{1,0:T(8,128)S(1)}, f32[184,128]{1,0:T(8,128)S(1)}, u32[]{:S(2)}, u32[]{:S(2)}) collective-permute-start(f32[184,128]{1,0:T(8,128)S(1)} %add.6), channel_id=1, source_target_pairs={{0,8},{4,12},{8,0},{12,4},{16,24},{20,28},{24,16},{28,20},{1,9},{5... | collective-permute-start | bytes 282632 | tf_op jit(solution)/shard_map/ppermute | solution.py:17
  14.3 5.6 %collective-permute-start.2 = (f32[184,128]{1,0:T(8,128)S(1)}, f32[184,128]{1,0:T(8,128)S(1)}, u32[]{:S(2)}, u32[]{:S(2)}) collective-permute-start(f32[184,128]{1,0:T(8,128)S(1)} %add.7.mine_ref), channel_id=1, source_target_pairs={{0,16},{4,20},{8,24},{12,28},{16,0},{20,4},{24,8},{28,12},{1,17},{... | collective-permute-start | bytes 282632 | tf_op jit(solution)/shard_map/ppermute | solution.py:17
  19.9 2.3 %collective-permute-start.3 = (bf16[48,512]{1,0:T(8,128)(2,1)S(1)}, bf16[48,512]{1,0:T(8,128)(2,1)S(1)}, u32[]{:S(2)}, u32[]{:S(2)}) collective-permute-start(bf16[48,512]{1,0:T(8,128)(2,1)S(1)} %finish.1.compact_ref), channel_id=1, source_target_pairs={{0,1},{1,0},{2,3},{3,2},{4,5},{5,4},{6,7},{7,6},{8,9},{9,8},{10,11... | collective-permute-start | bytes 147464 | tf_op jit(solution)/shard_map/ppermute | solution.py:17
  19.9 4.2 %collective-permute-start.4 = (bf16[48,512]{1,0:T(8,128)(2,1)S(1)}, bf16[48,512]{1,0:T(8,128)(2,1)S(1)}, u32[]{:S(2)}, u32[]{:S(2)}) collective-permute-start(bf16[48,512]{1,0:T(8,128)(2,1)S(1)} %finish.1.compact_ref), channel_id=1, source_target_pairs={{0,2},{1,3},{2,0},{3,1},{4,6},{5,7},{6,4},{7,5},{8,10},{9,11},{10,... | collective-permute-start | bytes 147464 | tf_op jit(solution)/shard_map/ppermute | solution.py:17
  24.2 1.2 %collective-permute-start.5 = (bf16[48,512]{1,0:T(8,128)(2,1)S(1)}, bf16[48,512]{1,0:T(8,128)(2,1)S(1)}, u32[]{:S(2)}, u32[]{:S(2)}) collective-permute-start(bf16[48,512]{1,0:T(8,128)(2,1)S(1)} %collective-permute-done.4.compact_ref), channel_id=1, source_target_pairs={{0,1},{1,0},{2,3},{3,2},{4,5},{5,4},{6,7},{7,6},{8,9},{9,8},{10,11... | collective-permute-start | bytes 147464 | tf_op jit(solution)/shard_map/ppermute | solution.py:17

commit v6 on v5

--- a/solution.py
+++ b/solution.py
@@ -211,20 +211,15 @@
         mine = mine + exchange(mine, "subj", subj, bit)
         bit *= 2
     pieces = {0: finish(mine, exchange(mine, "subj", subj, bit), voxel_cell_index, coef)}
-    pieces[1] = exchange(pieces[0], "slab", slab, 1)
-    dense = {o: place(coef, piece) for o, piece in pieces.items()}
-    bit = slab // 2
-    while bit > 1:
-        for o in [o for o in pieces if not o & 1]:
-            far = o ^ bit
-            pieces[far] = exchange(pieces[o], "slab", slab, bit)
-            dense, pieces[far] = lax.optimization_barrier((dense, pieces[far]))
-            pieces[far ^ 1] = exchange(pieces[far], "slab", slab, 1)
-            dense[far] = place(coef, pieces[far])
-            if len(pieces) < slab:
-                dense[far ^ 1] = place(coef, pieces[far ^ 1])
-        bit //= 2
-    return template(coef, (*dense, last := list(pieces)[-1]), list(dense.values()), pieces[last])
+    own = pieces[0]
+    for offset in reversed(range(1, slab)):
+        pieces[offset] = exchange(own, "slab", slab, offset)
+    last = slab // 2
+    order = [o for o in sorted(pieces) if o != last] + [last]
+    dense = []
+    for offset in order[:-1]:
+        dense.append(place(coef, pieces[offset]))
+    return template(coef, order, dense, pieces[last])
 
 
 def solution(mesh):

time: 26.6 us -> 27.1 us (1.019)
  waiting for transfers between devices: 10.4 us -> 10.7 us
    ppermute x6, waiting for transfers between devices: 10.4 us -> 10.7 us  [exchange(): return lax.ppermute(value, axis, [(i, i ^ bit) for i in range(size)])]
where the time goes in v6:
time: 27.1 us; the launch traced here: 27 us
  waiting for transfers between devices  10.7 us (39%)
  starting transfers between devices  10.2 us (38%)
  Pallas kernels  5.94 us (22%)
    ppermute x6, waiting for transfers between devices, exchange(): return lax.ppermute(value, axis, [(i, i ^ bit) for i in range(size)])  10.7 us
    ppermute x6, starting transfers between devices, exchange(): return lax.ppermute(value, axis, [(i, i ^ bit) for i in range(size)])  10.2 us
    pallas_call x1, Pallas kernels, local_sums(): pl.pallas_call(functools.partial(sums_kernel, subjects, chunk), out_shape...  3.81 us
    pallas_call x3, Pallas kernels, place(): pl.pallas_call(functools.partial(place_kernel, coef), out_shape=pltpu.VME...  1.06 us
    pallas_call x1, Pallas kernels, template(): pl.pallas_call(functools.partial(template_kernel, coef, order), out_shape...  1.03 us
  transfers between devices with their start and end apart: 6, of which 5 were waited for; matrix products, arithmetic and copies ran while one was open for 0% of the time, Pallas kernels for 4%

profile of v6, /device:TPU:0, one launch (start us, length us, event | category | flops | bytes accessed | tf_op | source)
XLA Modules:
  0.0 27.0 jit_solution(4508613652721513241)
XLA Ops:
  0.0 0.0 copy-start
  0.0 3.8 %local_sums.1 = f32[184,128]{1,0:T(8,128)S(1)} custom-call(bf16[45,45,16,128]{3,2,1,0:T(8,128)(2,1)} %bitcast.21, bf16[45,16,128]{2,1,0:T(8,128)(2,1)} %bitcast.22, f32[16,128]{1,0:T(8,128)} %bitcast.23, s32[4]{0:T(128)} %ids_hbm.1, f32[32]{0:T(128)} %study_hbm.1), custom_call_target="tpu_custom_call" | custom-call | tf_op jit(solution)/shard_map/local_sums/pallas_call | solution.py:94
  3.8 3.1 %collective-permute-start = (f32[184,128]{1,0:T(8,128)S(1)}, f32[184,128]{1,0:T(8,128)S(1)}, u32[]{:S(2)}, u32[]{:S(2)}) collective-permute-start(f32[184,128]{1,0:T(8,128)S(1)} %local_sums.1), channel_id=1, source_target_pairs={{0,4},{4,0},{8,12},{12,8},{16,20},{20,16},{24,28},{28,24},{1,5},{5... | collective-permute-start | bytes 282632 | tf_op jit(solution)/shard_map/ppermute | solution.py:17
  6.9 2.7 %collective-permute-done = f32[184,128]{1,0:T(8,128)S(1)} collective-permute-done((f32[184,128]{1,0:T(8,128)S(1)}, f32[184,128]{1,0:T(8,128)S(1)}, u32[]{:S(2)}, u32[]{:S(2)}) %collective-permute-start) | collective-permute-done | bytes 94240 | tf_op jit(solution)/shard_map/ppermute | solution.py:17
  9.6 2.0 %collective-permute-start.1 = (f32[184,128]{1,0:T(8,128)S(1)}, f32[184,128]{1,0:T(8,128)S(1)}, u32[]{:S(2)}, u32[]{:S(2)}) collective-permute-start(f32[184,128]{1,0:T(8,128)S(1)} %add.6), channel_id=1, source_target_pairs={{0,8},{4,12},{8,0},{12,4},{16,24},{20,28},{24,16},{28,20},{1,9},{5... | collective-permute-start | bytes 282632 | tf_op jit(solution)/shard_map/ppermute | solution.py:17
  11.6 2.6 %collective-permute-done.1 = f32[184,128]{1,0:T(8,128)S(1)} collective-permute-done((f32[184,128]{1,0:T(8,128)S(1)}, f32[184,128]{1,0:T(8,128)S(1)}, u32[]{:S(2)}, u32[]{:S(2)}) %collective-permute-start.1) | collective-permute-done | bytes 94240 | tf_op jit(solution)/shard_map/ppermute | solution.py:17
  14.3 3.0 %collective-permute-start.2 = (f32[184,128]{1,0:T(8,128)S(1)}, f32[184,128]{1,0:T(8,128)S(1)}, u32[]{:S(2)}, u32[]{:S(2)}) collective-permute-start(f32[184,128]{1,0:T(8,128)S(1)} %add.7.mine_ref), channel_id=1, source_target_pairs={{0,16},{4,20},{8,24},{12,28},{16,0},{20,4},{24,8},{28,12},{1,17},{... | collective-permute-start | bytes 282632 | tf_op jit(solution)/shard_map/ppermute | solution.py:17
  17.3 2.6 %collective-permute-done.2.other_ref = f32[184,128]{1,0:T(8,128)S(1)} collective-permute-done((f32[184,128]{1,0:T(8,128)S(1)}, f32[184,128]{1,0:T(8,128)S(1)}, u32[]{:S(2)}, u32[]{:S(2)}) %collective-permute-start.2) | collective-permute-done | bytes 94240 | tf_op jit(solution)/shard_map/ppermute | solution.py:17
  19.8 0.0 copy-done
  19.9 0.1 collective-permute-start.4
  19.9 1.9 %collective-permute-start.3 = (bf16[48,512]{1,0:T(8,128)(2,1)S(1)}, bf16[48,512]{1,0:T(8,128)(2,1)S(1)}, u32[]{:S(2)}, u32[]{:S(2)}) collective-permute-start(bf16[48,512]{1,0:T(8,128)(2,1)S(1)} %finish.1.compact_ref), channel_id=1, source_target_pairs={{0,1},{1,0},{2,3},{3,2},{4,5},{5,4},{6,7},{7,6},{8,9},{9,8},{10,11... | collective-permute-start | bytes 147464 | tf_op jit(solution)/shard_map/ppermute | solution.py:17
  21.9 0.2 collective-permute-start.5
  22.1 0.4 %place.3.refs_0_ = bf16[45,1024]{1,0:T(8,128)(2,1)S(1)} custom-call(bf16[48,512]{1,0:T(8,128)(2,1)S(1)} %finish.1.compact_ref), custom_call_target="tpu_custom_call" | custom-call | flops 47185920 | bytes 262144 | tf_op jit(solution)/shard_map/place/pallas_call | solution.py:165
  22.4 1.2 %collective-permute-done.4.compact_ref = bf16[48,512]{1,0:T(8,128)(2,1)S(1)} collective-permute-done((bf16[48,512]{1,0:T(8,128)(2,1)S(1)}, bf16[48,512]{1,0:T(8,128)(2,1)S(1)}, u32[]{:S(2)}, u32[]{:S(2)}) %collective-permute-start.4) | collective-permute-done | bytes 49184 | tf_op jit(solution)/shard_map/ppermute | solution.py:17
  23.6 0.4 %place.5.refs_2_ = bf16[45,1024]{1,0:T(8,128)(2,1)S(1)} custom-call(bf16[48,512]{1,0:T(8,128)(2,1)S(1)} %collective-permute-done.4.compact_ref), custom_call_target="tpu_custom_call" | custom-call | flops 47185920 | bytes 262144 | tf_op jit(solution)/shard_map/place/pallas_call | solution.py:165
  23.9 0.0 collective-permute-done.3.compact_ref
  24.0 0.4 %place.4.refs_1_ = bf16[45,1024]{1,0:T(8,128)(2,1)S(1)} custom-call(bf16[48,512]{1,0:T(8,128)(2,1)S(1)} %collective-permute-done.3.compact_ref), custom_call_target="tpu_custom_call" | custom-call | flops 47185920 | bytes 262144 | tf_op jit(solution)/shard_map/place/pallas_call | solution.py:165
  24.3 1.6 %collective-permute-done.5.refs_3_ = bf16[48,512]{1,0:T(8,128)(2,1)S(1)} collective-permute-done((bf16[48,512]{1,0:T(8,128)(2,1)S(1)}, bf16[48,512]{1,0:T(8,128)(2,1)S(1)}, u32[]{:S(2)}, u32[]{:S(2)}) %collective-permute-start.5) | collective-permute-done | bytes 49184 | tf_op jit(solution)/shard_map/ppermute | solution.py:17
  25.9 1.0 %template.1 = bf16[45,4096]{1,0:T(8,128)(2,1)} custom-call(bf16[45,1024]{1,0:T(8,128)(2,1)S(1)} %place.3.refs_0_, bf16[45,1024]{1,0:T(8,128)(2,1)S(1)} %place.4.refs_1_, bf16[45,1024]{1,0:T(8,128)(2,1)S(1)} %place.5.refs_2_, bf16[48,512]{1,0:T(8,128)(2,1)S(1)} %collective-permute-done.5.refs_3_), custom_call_target="tpu_custom_call" | custom-call | tf_op jit(solution)/shard_map/template/pallas_call | solution.py:195
  (3 shorter events, 0.1 us)
Async XLA Ops:
  0.0 19.8 %copy-start = (s32[512]{0:T(512)S(1)}, s32[512]{0:T(512)}, u32[]{:S(2)}) copy-start(s32[512]{0:T(512)} %param.11) | copy-start | bytes 6148
  3.8 5.8 %collective-permute-start = (f32[184,128]{1,0:T(8,128)S(1)}, f32[184,128]{1,0:T(8,128)S(1)}, u32[]{:S(2)}, u32[]{:S(2)}) collective-permute-start(f32[184,128]{1,0:T(8,128)S(1)} %local_sums.1), channel_id=1, source_target_pairs={{0,4},{4,0},{8,12},{12,8},{16,20},{20,16},{24,28},{28,24},{1,5},{5... | collective-permute-start | bytes 282632 | tf_op jit(solution)/shard_map/ppermute | solution.py:17
  9.6 4.6 %collective-permute-start.1 = (f32[184,128]{1,0:T(8,128)S(1)}, f32[184,128]{1,0:T(8,128)S(1)}, u32[]{:S(2)}, u32[]{:S(2)}) collective-permute-start(f32[184,128]{1,0:T(8,128)S(1)} %add.6), channel_id=1, source_target_pairs={{0,8},{4,12},{8,0},{12,4},{16,24},{20,28},{24,16},{28,20},{1,9},{5... | collective-permute-start | bytes 282632 | tf_op jit(solution)/shard_map/ppermute | solution.py:17
  14.3 5.6 %collective-permute-start.2 = (f32[184,128]{1,0:T(8,128)S(1)}, f32[184,128]{1,0:T(8,128)S(1)}, u32[]{:S(2)}, u32[]{:S(2)}) collective-permute-start(f32[184,128]{1,0:T(8,128)S(1)} %add.7.mine_ref), channel_id=1, source_target_pairs={{0,16},{4,20},{8,24},{12,28},{16,0},{20,4},{24,8},{28,12},{1,17},{... | collective-permute-start | bytes 282632 | tf_op jit(solution)/shard_map/ppermute | solution.py:17
  19.9 3.7 %collective-permute-start.4 = (bf16[48,512]{1,0:T(8,128)(2,1)S(1)}, bf16[48,512]{1,0:T(8,128)(2,1)S(1)}, u32[]{:S(2)}, u32[]{:S(2)}) collective-permute-start(bf16[48,512]{1,0:T(8,128)(2,1)S(1)} %finish.1.compact_ref), channel_id=1, source_target_pairs={{0,3},{1,2},{2,1},{3,0},{4,7},{5,6},{6,5},{7,4},{8,11},{9,10},{10,... | collective-permute-start | bytes 147464 | tf_op jit(solution)/shard_map/ppermute | solution.py:17
  19.9 4.0 %collective-permute-start.3 = (bf16[48,512]{1,0:T(8,128)(2,1)S(1)}, bf16[48,512]{1,0:T(8,128)(2,1)S(1)}, u32[]{:S(2)}, u32[]{:S(2)}) collective-permute-start(bf16[48,512]{1,0:T(8,128)(2,1)S(1)} %finish.1.compact_ref), channel_id=1, source_target_pairs={{0,1},{1,0},{2,3},{3,2},{4,5},{5,4},{6,7},{7,6},{8,9},{9,8},{10,11... | collective-permute-start | bytes 147464 | tf_op jit(solution)/shard_map/ppermute | solution.py:17
  21.9 4.1 %collective-permute-start.5 = (bf16[48,512]{1,0:T(8,128)(2,1)S(1)}, bf16[48,512]{1,0:T(8,128)(2,1)S(1)}, u32[]{:S(2)}, u32[]{:S(2)}) collective-permute-start(bf16[48,512]{1,0:T(8,128)(2,1)S(1)} %finish.1.compact_ref), channel_id=1, source_target_pairs={{0,2},{1,3},{2,0},{3,1},{4,6},{5,7},{6,4},{7,5},{8,10},{9,11},{10,... | collective-permute-start | bytes 147464 | tf_op jit(solution)/shard_map/ppermute | solution.py:17

commit v7 on v6

--- a/solution.py
+++ b/solution.py
@@ -15,6 +15,11 @@
 
 def exchange(value, axis, size, bit):
     return lax.ppermute(value, axis, [(i, i ^ bit) for i in range(size)])
+
+
+def exchange_by_core(value, subj, slab, even, odd):
+    pairs = [(i * slab + j, (i ^ (odd if j & 1 else even)) * slab + j) for i in range(subj) for j in range(slab)]
+    return lax.ppermute(value, ("subj", "slab"), pairs)
 
 
 def sums_kernel(
@@ -112,10 +117,14 @@
     )(*[pltpu.with_memory_space_constraint(x, pltpu.HBM) for x in (turned, fod, modulation, subject_ids, subject_weight)])
 
 
-def finish_kernel(coef, mine_ref, other_ref, cells_ref, out_ref, total):
+def finish_kernel(coef, terms, *refs):
+    parts, (cells_ref, out_ref, total) = refs[:terms], refs[terms:]
     rows, voxels = out_ref.shape
     blocks = voxels // LANES
-    total[pl.ds(0, mine_ref.shape[0])] = mine_ref[...] + other_ref[...]
+    values = [part[...] for part in parts]
+    while len(values) > 1:
+        values = [values[i] + values[i + 1] for i in range(0, len(values), 2)]
+    total[pl.ds(0, parts[0].shape[0])] = values[0]
     row = lax.broadcasted_iota(jnp.int32, (rows, LANES), 0)
     for block in range(blocks):
         numer = total[pl.ds(block, rows, stride=blocks)]
@@ -126,18 +135,18 @@
         out_ref[:, pl.ds(block * LANES, LANES)] = value.astype(jnp.bfloat16)
 
 
-def finish(mine, other, cells, coef):
+def finish(parts, cells, coef):
     blocks = cells.shape[0] // LANES
     rows = -(-(coef + 2) // 8) * 8
     return pl.pallas_call(
-        functools.partial(finish_kernel, coef),
+        functools.partial(finish_kernel, coef, len(parts)),
         out_shape=pltpu.VMEM((rows, cells.shape[0]), jnp.bfloat16),
-        in_specs=[pl.BlockSpec(memory_space=pltpu.VMEM)] * 3,
+        in_specs=[pl.BlockSpec(memory_space=pltpu.VMEM)] * (len(parts) + 1),
         out_specs=pl.BlockSpec(memory_space=pltpu.VMEM),
         scratch_shapes=[pltpu.VMEM((rows * blocks, LANES), jnp.float32)],
         compiler_params=pltpu.CompilerParams(vmem_limit_bytes=16 << 20),
         name="finish",
-    )(mine, other, cells.reshape(blocks, LANES))
+    )(*parts, cells.reshape(blocks, LANES))
 
 
 def dense_of(coef, compact):
@@ -206,12 +215,17 @@
 def on_device(subj, slab, fod, rotation, modulation, subject_ids, subject_weight, voxel_cell_index):
     coef = fod.shape[1]
     mine = local_sums(fod, rotation, modulation, subject_ids, subject_weight)
-    bit = 1
-    while 2 * bit < subj:
-        mine = mine + exchange(mine, "subj", subj, bit)
-        bit *= 2
-    pieces = {0: finish(mine, exchange(mine, "subj", subj, bit), voxel_cell_index, coef)}
-    own = pieces[0]
+    count = subj.bit_length() - 1
+    bits = [1 << n for n in range(count)]
+    even, odd = [bits[-1], *bits[:-1]], [bits[-2], *bits[:-2], bits[-1]]
+    for one, other in zip(even[:-2], odd[:-2]):
+        mine = mine + exchange_by_core(mine, subj, slab, one, other)
+    parts = [mine]
+    for pick in ((0,), (1,), (0, 1)):
+        offsets = [sum(order[-2:][n] for n in pick) for order in (even, odd)]
+        parts.append(exchange_by_core(mine, subj, slab, *offsets))
+    own = finish(parts, voxel_cell_index, coef)
+    pieces = {0: own}
     for offset in reversed(range(1, slab)):
         pieces[offset] = exchange(own, "slab", slab, offset)
     last = slab // 2

time: 27.1 us -> 25.5 us (0.941)
  waiting for transfers between devices: 10.7 us -> 9.29 us
    ppermute x6 -> x3, waiting for transfers between devices: 10.7 us -> 2.46 us  [exchange(): return lax.ppermute(value, axis, [(i, i ^ bit) for i in range(size)])]
    ppermute x6 -> x3, starting transfers between devices: 10.2 us -> 2.2 us  [exchange(): return lax.ppermute(value, axis, [(i, i ^ bit) for i in range(size)])]
    ppermute x0 -> x4, starting transfers between devices: none -> 7.8 us  [exchange_by_core(): return lax.ppermute(value, ('subj', 'slab'), pairs)]
    ppermute x0 -> x4, waiting for transfers between devices: none -> 6.83 us  [exchange_by_core(): return lax.ppermute(value, ('subj', 'slab'), pairs)]
  transfers between devices with their start and end apart: 6 -> 7, of which waited for: 5 -> 5; matrix products, arithmetic and copies ran while one was open for 0% -> 0% of each run, Pallas kernels for 4% -> 4%
where the time goes in v7:
time: 25.5 us; the launch traced here: 25.3 us
  starting transfers between devices  10 us (39%)
  waiting for transfers between devices  9.29 us (36%)
  Pallas kernels  5.96 us (23%)
    ppermute x4, starting transfers between devices, exchange_by_core(): return lax.ppermute(value, ('subj', 'slab'), pairs)  7.8 us
    ppermute x4, waiting for transfers between devices, exchange_by_core(): return lax.ppermute(value, ('subj', 'slab'), pairs)  6.83 us
    pallas_call x1, Pallas kernels, local_sums(): pl.pallas_call(functools.partial(sums_kernel, subjects, chunk), out_shape...  3.81 us
    ppermute x3, waiting for transfers between devices, exchange(): return lax.ppermute(value, axis, [(i, i ^ bit) for i in range(size)])  2.46 us
    ppermute x3, starting transfers between devices, exchange(): return lax.ppermute(value, axis, [(i, i ^ bit) for i in range(size)])  2.2 us
    pallas_call x3, Pallas kernels, place(): pl.pallas_call(functools.partial(place_kernel, coef), out_shape=pltpu.VME...  1.06 us
    pallas_call x1, Pallas kernels, template(): pl.pallas_call(functools.partial(template_kernel, coef, order), out_shape...  1.03 us
  transfers between devices with their start and end apart: 7, of which 5 were waited for; matrix products, arithmetic and copies ran while one was open for 0% of the time, Pallas kernels for 4%

profile of v7, /device:TPU:0, one launch (start us, length us, event | category | flops | bytes accessed | tf_op | source)
XLA Modules:
  0.0 25.3 jit_solution(7043884927115727576)
XLA Ops:
  0.0 0.0 copy-start
  0.0 3.8 %local_sums.1 = f32[184,128]{1,0:T(8,128)S(1)} custom-call(bf16[45,45,16,128]{3,2,1,0:T(8,128)(2,1)} %bitcast.21, bf16[45,16,128]{2,1,0:T(8,128)(2,1)} %bitcast.22, f32[16,128]{1,0:T(8,128)} %bitcast.23, s32[4]{0:T(128)} %ids_hbm.1, f32[32]{0:T(128)} %study_hbm.1), custom_call_target="tpu_custom_call" | custom-call | tf_op jit(solution)/shard_map/local_sums/pallas_call | solution.py:99
  3.8 4.1 %collective-permute-start = (f32[184,128]{1,0:T(8,128)S(1)}, f32[184,128]{1,0:T(8,128)S(1)}, u32[]{:S(2)}, u32[]{:S(2)}) collective-permute-start(f32[184,128]{1,0:T(8,128)S(1)} %local_sums.1), channel_id=1, source_target_pairs={{0,16},{1,9},{2,18},{3,11},{4,20},{5,13},{6,22},{7,15},{8,24},{9,1... | collective-permute-start | bytes 282632 | tf_op jit(solution)/shard_map/ppermute | solution.py:22
  7.9 2.6 %collective-permute-done = f32[184,128]{1,0:T(8,128)S(1)} collective-permute-done((f32[184,128]{1,0:T(8,128)S(1)}, f32[184,128]{1,0:T(8,128)S(1)}, u32[]{:S(2)}, u32[]{:S(2)}) %collective-permute-start) | collective-permute-done | bytes 94240 | tf_op jit(solution)/shard_map/ppermute | solution.py:22
  10.5 3.0 %collective-permute-start.3 = (f32[184,128]{1,0:T(8,128)S(1)}, f32[184,128]{1,0:T(8,128)S(1)}, u32[]{:S(2)}, u32[]{:S(2)}) collective-permute-start(f32[184,128]{1,0:T(8,128)S(1)} %add.3.refs_0_), channel_id=1, source_target_pairs={{0,12},{1,21},{2,14},{3,23},{4,8},{5,17},{6,10},{7,19},{8,4},{9,29... | collective-permute-start | bytes 282632 | tf_op jit(solution)/shard_map/ppermute | solution.py:22
  13.5 0.3 %collective-permute-start.2 = (f32[184,128]{1,0:T(8,128)S(1)}, f32[184,128]{1,0:T(8,128)S(1)}, u32[]{:S(2)}, u32[]{:S(2)}) collective-permute-start(f32[184,128]{1,0:T(8,128)S(1)} %add.3.refs_0_), channel_id=1, source_target_pairs={{0,8},{1,17},{2,10},{3,19},{4,12},{5,21},{6,14},{7,23},{8,0},{9,25... | collective-permute-start | bytes 282632 | tf_op jit(solution)/shard_map/ppermute | solution.py:22
  13.9 0.3 %collective-permute-start.1 = (f32[184,128]{1,0:T(8,128)S(1)}, f32[184,128]{1,0:T(8,128)S(1)}, u32[]{:S(2)}, u32[]{:S(2)}) collective-permute-start(f32[184,128]{1,0:T(8,128)S(1)} %add.3.refs_0_), channel_id=1, source_target_pairs={{0,4},{1,5},{2,6},{3,7},{4,0},{5,1},{6,2},{7,3},{8,12},{9,13},{10,... | collective-permute-start | bytes 282632 | tf_op jit(solution)/shard_map/ppermute | solution.py:22
  14.2 2.9 %collective-permute-done.3.refs_3_ = f32[184,128]{1,0:T(8,128)S(1)} collective-permute-done((f32[184,128]{1,0:T(8,128)S(1)}, f32[184,128]{1,0:T(8,128)S(1)}, u32[]{:S(2)}, u32[]{:S(2)}) %collective-permute-start.3) | collective-permute-done | bytes 94240 | tf_op jit(solution)/shard_map/ppermute | solution.py:22
  17.1 1.3 %collective-permute-done.2.refs_2_ = f32[184,128]{1,0:T(8,128)S(1)} collective-permute-done((f32[184,128]{1,0:T(8,128)S(1)}, f32[184,128]{1,0:T(8,128)S(1)}, u32[]{:S(2)}, u32[]{:S(2)}) %collective-permute-start.2) | collective-permute-done | bytes 94240 | tf_op jit(solution)/shard_map/ppermute | solution.py:22
  18.5 0.0 collective-permute-done.1.refs_1_
  18.5 0.0 copy-done
  18.5 0.1 finish.1.compact_ref
  18.5 0.1 collective-permute-start.5
  18.6 1.6 %collective-permute-start.4 = (bf16[48,512]{1,0:T(8,128)(2,1)S(1)}, bf16[48,512]{1,0:T(8,128)(2,1)S(1)}, u32[]{:S(2)}, u32[]{:S(2)}) collective-permute-start(bf16[48,512]{1,0:T(8,128)(2,1)S(1)} %finish.1.compact_ref), channel_id=1, source_target_pairs={{0,1},{1,0},{2,3},{3,2},{4,5},{5,4},{6,7},{7,6},{8,9},{9,8},{10,11... | collective-permute-start | bytes 147464 | tf_op jit(solution)/shard_map/ppermute | solution.py:17
  20.2 0.5 %collective-permute-start.6 = (bf16[48,512]{1,0:T(8,128)(2,1)S(1)}, bf16[48,512]{1,0:T(8,128)(2,1)S(1)}, u32[]{:S(2)}, u32[]{:S(2)}) collective-permute-start(bf16[48,512]{1,0:T(8,128)(2,1)S(1)} %finish.1.compact_ref), channel_id=1, source_target_pairs={{0,2},{1,3},{2,0},{3,1},{4,6},{5,7},{6,4},{7,5},{8,10},{9,11},{10,... | collective-permute-start | bytes 147464 | tf_op jit(solution)/shard_map/ppermute | solution.py:17
  20.7 0.4 %place.3.refs_0_ = bf16[45,1024]{1,0:T(8,128)(2,1)S(1)} custom-call(bf16[48,512]{1,0:T(8,128)(2,1)S(1)} %finish.1.compact_ref), custom_call_target="tpu_custom_call" | custom-call | flops 47185920 | bytes 262144 | tf_op jit(solution)/shard_map/place/pallas_call | solution.py:174
  21.1 1.5 %collective-permute-done.5.compact_ref = bf16[48,512]{1,0:T(8,128)(2,1)S(1)} collective-permute-done((bf16[48,512]{1,0:T(8,128)(2,1)S(1)}, bf16[48,512]{1,0:T(8,128)(2,1)S(1)}, u32[]{:S(2)}, u32[]{:S(2)}) %collective-permute-start.5) | collective-permute-done | bytes 49184 | tf_op jit(solution)/shard_map/ppermute | solution.py:17
  22.6 0.4 %place.5.refs_2_ = bf16[45,1024]{1,0:T(8,128)(2,1)S(1)} custom-call(bf16[48,512]{1,0:T(8,128)(2,1)S(1)} %collective-permute-done.5.compact_ref), custom_call_target="tpu_custom_call" | custom-call | flops 47185920 | bytes 262144 | tf_op jit(solution)/shard_map/place/pallas_call | solution.py:174
  22.9 0.0 collective-permute-done.4.compact_ref
  23.0 0.4 %place.4.refs_1_ = bf16[45,1024]{1,0:T(8,128)(2,1)S(1)} custom-call(bf16[48,512]{1,0:T(8,128)(2,1)S(1)} %collective-permute-done.4.compact_ref), custom_call_target="tpu_custom_call" | custom-call | flops 47185920 | bytes 262144 | tf_op jit(solution)/shard_map/place/pallas_call | solution.py:174
  23.3 1.0 %collective-permute-done.6.refs_3_ = bf16[48,512]{1,0:T(8,128)(2,1)S(1)} collective-permute-done((bf16[48,512]{1,0:T(8,128)(2,1)S(1)}, bf16[48,512]{1,0:T(8,128)(2,1)S(1)}, u32[]{:S(2)}, u32[]{:S(2)}) %collective-permute-start.6) | collective-permute-done | bytes 49184 | tf_op jit(solution)/shard_map/ppermute | solution.py:17
  24.3 1.0 %template.1 = bf16[45,4096]{1,0:T(8,128)(2,1)} custom-call(bf16[45,1024]{1,0:T(8,128)(2,1)S(1)} %place.3.refs_0_, bf16[45,1024]{1,0:T(8,128)(2,1)S(1)} %place.4.refs_1_, bf16[45,1024]{1,0:T(8,128)(2,1)S(1)} %place.5.refs_2_, bf16[48,512]{1,0:T(8,128)(2,1)S(1)} %collective-permute-done.6.refs_3_), custom_call_target="tpu_custom_call" | custom-call | tf_op jit(solution)/shard_map/template/pallas_call | solution.py:204
  (1 shorter events, 0.0 us)
Async XLA Ops:
  0.0 18.5 %copy-start = (s32[512]{0:T(512)S(1)}, s32[512]{0:T(512)}, u32[]{:S(2)}) copy-start(s32[512]{0:T(512)} %param.11) | copy-start | bytes 6148
  3.8 6.7 %collective-permute-start = (f32[184,128]{1,0:T(8,128)S(1)}, f32[184,128]{1,0:T(8,128)S(1)}, u32[]{:S(2)}, u32[]{:S(2)}) collective-permute-start(f32[184,128]{1,0:T(8,128)S(1)} %local_sums.1), channel_id=1, source_target_pairs={{0,16},{1,9},{2,18},{3,11},{4,20},{5,13},{6,22},{7,15},{8,24},{9,1... | collective-permute-start | bytes 282632 | tf_op jit(solution)/shard_map/ppermute | solution.py:22
  10.5 6.6 %collective-permute-start.3 = (f32[184,128]{1,0:T(8,128)S(1)}, f32[184,128]{1,0:T(8,128)S(1)}, u32[]{:S(2)}, u32[]{:S(2)}) collective-permute-start(f32[184,128]{1,0:T(8,128)S(1)} %add.3.refs_0_), channel_id=1, source_target_pairs={{0,12},{1,21},{2,14},{3,23},{4,8},{5,17},{6,10},{7,19},{8,4},{9,29... | collective-permute-start | bytes 282632 | tf_op jit(solution)/shard_map/ppermute | solution.py:22
  13.5 4.9 %collective-permute-start.2 = (f32[184,128]{1,0:T(8,128)S(1)}, f32[184,128]{1,0:T(8,128)S(1)}, u32[]{:S(2)}, u32[]{:S(2)}) collective-permute-start(f32[184,128]{1,0:T(8,128)S(1)} %add.3.refs_0_), channel_id=1, source_target_pairs={{0,8},{1,17},{2,10},{3,19},{4,12},{5,21},{6,14},{7,23},{8,0},{9,25... | collective-permute-start | bytes 282632 | tf_op jit(solution)/shard_map/ppermute | solution.py:22
  13.9 4.6 %collective-permute-start.1 = (f32[184,128]{1,0:T(8,128)S(1)}, f32[184,128]{1,0:T(8,128)S(1)}, u32[]{:S(2)}, u32[]{:S(2)}) collective-permute-start(f32[184,128]{1,0:T(8,128)S(1)} %add.3.refs_0_), channel_id=1, source_target_pairs={{0,4},{1,5},{2,6},{3,7},{4,0},{5,1},{6,2},{7,3},{8,12},{9,13},{10,... | collective-permute-start | bytes 282632 | tf_op jit(solution)/shard_map/ppermute | solution.py:22
  18.5 4.1 %collective-permute-start.5 = (bf16[48,512]{1,0:T(8,128)(2,1)S(1)}, bf16[48,512]{1,0:T(8,128)(2,1)S(1)}, u32[]{:S(2)}, u32[]{:S(2)}) collective-permute-start(bf16[48,512]{1,0:T(8,128)(2,1)S(1)} %finish.1.compact_ref), channel_id=1, source_target_pairs={{0,3},{1,2},{2,1},{3,0},{4,7},{5,6},{6,5},{7,4},{8,11},{9,10},{10,... | collective-permute-start | bytes 147464 | tf_op jit(solution)/shard_map/ppermute | solution.py:17
  18.6 4.3 %collective-permute-start.4 = (bf16[48,512]{1,0:T(8,128)(2,1)S(1)}, bf16[48,512]{1,0:T(8,128)(2,1)S(1)}, u32[]{:S(2)}, u32[]{:S(2)}) collective-permute-start(bf16[48,512]{1,0:T(8,128)(2,1)S(1)} %finish.1.compact_ref), channel_id=1, source_target_pairs={{0,1},{1,0},{2,3},{3,2},{4,5},{5,4},{6,7},{7,6},{8,9},{9,8},{10,11... | collective-permute-start | bytes 147464 | tf_op jit(solution)/shard_map/ppermute | solution.py:17
  20.2 4.1 %collective-permute-start.6 = (bf16[48,512]{1,0:T(8,128)(2,1)S(1)}, bf16[48,512]{1,0:T(8,128)(2,1)S(1)}, u32[]{:S(2)}, u32[]{:S(2)}) collective-permute-start(bf16[48,512]{1,0:T(8,128)(2,1)S(1)} %finish.1.compact_ref), channel_id=1, source_target_pairs={{0,2},{1,3},{2,0},{3,1},{4,6},{5,7},{6,4},{7,5},{8,10},{9,11},{10,... | collective-permute-start | bytes 147464 | tf_op jit(solution)/shard_map/ppermute | solution.py:17

commit v8 on v7

--- a/solution.py
+++ b/solution.py
@@ -48,8 +48,6 @@
         pltpu.make_async_copy(modulation_hbm, modulation, small_sem.at[2]),
         pltpu.make_async_copy(fod_hbm, fod, small_sem.at[3]),
     ]
-    for copy in small:
-        copy.start()
 
     def big(step):
         part = pl.ds(step * chunk, chunk)
@@ -57,6 +55,8 @@
 
     for step in range(coef // chunk):
         big(step).start(priority=1)
+    for copy in small:
+        copy.start()
     for copy in small:
         copy.wait()
 
@@ -153,13 +153,13 @@
     voxels = compact.shape[1]
     high = compact[coef : coef + 1].astype(jnp.float32)
     low = compact[coef + 1 : coef + 2].astype(jnp.float32)
-    cells = (high * SPLIT + low).astype(jnp.int32)
+    cells = (high * SPLIT + low).astype(jnp.int32).astype(jnp.int16)
     tiles = []
     for start in range(0, GRID_DEV, TILE):
         first = max(start - (GRID_DEV - voxels), 0) // TILE * TILE
         last = min(start + TILE, voxels)
-        hit = lax.broadcasted_iota(jnp.int32, (TILE, last - first), 0) + start == cells[:, first:last]
-        onehot = jnp.where(hit, 1.0, 0.0).astype(jnp.bfloat16)
+        hit = lax.broadcasted_iota(jnp.int16, (TILE, last - first), 0) + jnp.int16(start) == cells[:, first:last]
+        onehot = jnp.where(hit, jnp.bfloat16(1), jnp.bfloat16(0))
         tiles.append(
             lax.dot_general(compact[:, first:last], onehot, (((1,), (1,)), ((), ())), preferred_element_type=jnp.float32)
         )

time: 25.5 us -> 25.5 us (level)
  no operation moved by 1% of the time
where the time goes in v8:
time: 25.5 us; the launch traced here: 25.3 us
  starting transfers between devices  10 us (39%)
  waiting for transfers between devices  9.28 us (36%)
  Pallas kernels  5.97 us (23%)
    ppermute x4, starting transfers between devices, exchange_by_core(): return lax.ppermute(value, ('subj', 'slab'), pairs)  7.8 us
    ppermute x4, waiting for transfers between devices, exchange_by_core(): return lax.ppermute(value, ('subj', 'slab'), pairs)  6.83 us
    pallas_call x1, Pallas kernels, local_sums(): pl.pallas_call(functools.partial(sums_kernel, subjects, chunk), out_shape...  3.81 us
    ppermute x3, waiting for transfers between devices, exchange(): return lax.ppermute(value, axis, [(i, i ^ bit) for i in range(size)])  2.45 us
    ppermute x3, starting transfers between devices, exchange(): return lax.ppermute(value, axis, [(i, i ^ bit) for i in range(size)])  2.2 us
    pallas_call x3, Pallas kernels, place(): pl.pallas_call(functools.partial(place_kernel, coef), out_shape=pltpu.VME...  1.07 us
    pallas_call x1, Pallas kernels, template(): pl.pallas_call(functools.partial(template_kernel, coef, order), out_shape...  1.04 us
  transfers between devices with their start and end apart: 7, of which 5 were waited for; matrix products, arithmetic and copies ran while one was open for 0% of the time, Pallas kernels for 4%

profile of v8, /device:TPU:0, one launch (start us, length us, event | category | flops | bytes accessed | tf_op | source)
XLA Modules:
  0.0 25.3 jit_solution(873086614752635832)
XLA Ops:
  0.0 0.0 copy-start
  0.0 3.8 %local_sums.1 = f32[184,128]{1,0:T(8,128)S(1)} custom-call(bf16[45,45,16,128]{3,2,1,0:T(8,128)(2,1)} %bitcast.21, bf16[45,16,128]{2,1,0:T(8,128)(2,1)} %bitcast.22, f32[16,128]{1,0:T(8,128)} %bitcast.23, s32[4]{0:T(128)} %ids_hbm.1, f32[32]{0:T(128)} %study_hbm.1), custom_call_target="tpu_custom_call" | custom-call | tf_op jit(solution)/shard_map/local_sums/pallas_call | solution.py:99
  3.8 4.1 %collective-permute-start = (f32[184,128]{1,0:T(8,128)S(1)}, f32[184,128]{1,0:T(8,128)S(1)}, u32[]{:S(2)}, u32[]{:S(2)}) collective-permute-start(f32[184,128]{1,0:T(8,128)S(1)} %local_sums.1), channel_id=1, source_target_pairs={{0,16},{1,9},{2,18},{3,11},{4,20},{5,13},{6,22},{7,15},{8,24},{9,1... | collective-permute-start | bytes 282632 | tf_op jit(solution)/shard_map/ppermute | solution.py:22
  7.9 2.6 %collective-permute-done = f32[184,128]{1,0:T(8,128)S(1)} collective-permute-done((f32[184,128]{1,0:T(8,128)S(1)}, f32[184,128]{1,0:T(8,128)S(1)}, u32[]{:S(2)}, u32[]{:S(2)}) %collective-permute-start) | collective-permute-done | bytes 94240 | tf_op jit(solution)/shard_map/ppermute | solution.py:22
  10.5 3.0 %collective-permute-start.3 = (f32[184,128]{1,0:T(8,128)S(1)}, f32[184,128]{1,0:T(8,128)S(1)}, u32[]{:S(2)}, u32[]{:S(2)}) collective-permute-start(f32[184,128]{1,0:T(8,128)S(1)} %add.3.refs_0_), channel_id=1, source_target_pairs={{0,12},{1,21},{2,14},{3,23},{4,8},{5,17},{6,10},{7,19},{8,4},{9,29... | collective-permute-start | bytes 282632 | tf_op jit(solution)/shard_map/ppermute | solution.py:22
  13.5 0.3 %collective-permute-start.2 = (f32[184,128]{1,0:T(8,128)S(1)}, f32[184,128]{1,0:T(8,128)S(1)}, u32[]{:S(2)}, u32[]{:S(2)}) collective-permute-start(f32[184,128]{1,0:T(8,128)S(1)} %add.3.refs_0_), channel_id=1, source_target_pairs={{0,8},{1,17},{2,10},{3,19},{4,12},{5,21},{6,14},{7,23},{8,0},{9,25... | collective-permute-start | bytes 282632 | tf_op jit(solution)/shard_map/ppermute | solution.py:22
  13.9 0.3 %collective-permute-start.1 = (f32[184,128]{1,0:T(8,128)S(1)}, f32[184,128]{1,0:T(8,128)S(1)}, u32[]{:S(2)}, u32[]{:S(2)}) collective-permute-start(f32[184,128]{1,0:T(8,128)S(1)} %add.3.refs_0_), channel_id=1, source_target_pairs={{0,4},{1,5},{2,6},{3,7},{4,0},{5,1},{6,2},{7,3},{8,12},{9,13},{10,... | collective-permute-start | bytes 282632 | tf_op jit(solution)/shard_map/ppermute | solution.py:22
  14.2 2.9 %collective-permute-done.3.refs_3_ = f32[184,128]{1,0:T(8,128)S(1)} collective-permute-done((f32[184,128]{1,0:T(8,128)S(1)}, f32[184,128]{1,0:T(8,128)S(1)}, u32[]{:S(2)}, u32[]{:S(2)}) %collective-permute-start.3) | collective-permute-done | bytes 94240 | tf_op jit(solution)/shard_map/ppermute | solution.py:22
  17.1 1.3 %collective-permute-done.2.refs_2_ = f32[184,128]{1,0:T(8,128)S(1)} collective-permute-done((f32[184,128]{1,0:T(8,128)S(1)}, f32[184,128]{1,0:T(8,128)S(1)}, u32[]{:S(2)}, u32[]{:S(2)}) %collective-permute-start.2) | collective-permute-done | bytes 94240 | tf_op jit(solution)/shard_map/ppermute | solution.py:22
  18.5 0.0 collective-permute-done.1.refs_1_
  18.5 0.0 copy-done
  18.5 0.1 finish.1.compact_ref
  18.5 0.1 collective-permute-start.5
  18.6 1.6 %collective-permute-start.4 = (bf16[48,512]{1,0:T(8,128)(2,1)S(1)}, bf16[48,512]{1,0:T(8,128)(2,1)S(1)}, u32[]{:S(2)}, u32[]{:S(2)}) collective-permute-start(bf16[48,512]{1,0:T(8,128)(2,1)S(1)} %finish.1.compact_ref), channel_id=1, source_target_pairs={{0,1},{1,0},{2,3},{3,2},{4,5},{5,4},{6,7},{7,6},{8,9},{9,8},{10,11... | collective-permute-start | bytes 147464 | tf_op jit(solution)/shard_map/ppermute | solution.py:17
  20.2 0.5 %collective-permute-start.6 = (bf16[48,512]{1,0:T(8,128)(2,1)S(1)}, bf16[48,512]{1,0:T(8,128)(2,1)S(1)}, u32[]{:S(2)}, u32[]{:S(2)}) collective-permute-start(bf16[48,512]{1,0:T(8,128)(2,1)S(1)} %finish.1.compact_ref), channel_id=1, source_target_pairs={{0,2},{1,3},{2,0},{3,1},{4,6},{5,7},{6,4},{7,5},{8,10},{9,11},{10,... | collective-permute-start | bytes 147464 | tf_op jit(solution)/shard_map/ppermute | solution.py:17
  20.7 0.4 %place.3.refs_0_ = bf16[45,1024]{1,0:T(8,128)(2,1)S(1)} custom-call(bf16[48,512]{1,0:T(8,128)(2,1)S(1)} %finish.1.compact_ref), custom_call_target="tpu_custom_call" | custom-call | flops 47185920 | bytes 262144 | tf_op jit(solution)/shard_map/place/pallas_call | solution.py:174
  21.1 1.5 %collective-permute-done.5.compact_ref = bf16[48,512]{1,0:T(8,128)(2,1)S(1)} collective-permute-done((bf16[48,512]{1,0:T(8,128)(2,1)S(1)}, bf16[48,512]{1,0:T(8,128)(2,1)S(1)}, u32[]{:S(2)}, u32[]{:S(2)}) %collective-permute-start.5) | collective-permute-done | bytes 49184 | tf_op jit(solution)/shard_map/ppermute | solution.py:17
  22.6 0.4 %place.5.refs_2_ = bf16[45,1024]{1,0:T(8,128)(2,1)S(1)} custom-call(bf16[48,512]{1,0:T(8,128)(2,1)S(1)} %collective-permute-done.5.compact_ref), custom_call_target="tpu_custom_call" | custom-call | flops 47185920 | bytes 262144 | tf_op jit(solution)/shard_map/place/pallas_call | solution.py:174
  22.9 0.0 collective-permute-done.4.compact_ref
  23.0 0.4 %place.4.refs_1_ = bf16[45,1024]{1,0:T(8,128)(2,1)S(1)} custom-call(bf16[48,512]{1,0:T(8,128)(2,1)S(1)} %collective-permute-done.4.compact_ref), custom_call_target="tpu_custom_call" | custom-call | flops 47185920 | bytes 262144 | tf_op jit(solution)/shard_map/place/pallas_call | solution.py:174
  23.3 1.0 %collective-permute-done.6.refs_3_ = bf16[48,512]{1,0:T(8,128)(2,1)S(1)} collective-permute-done((bf16[48,512]{1,0:T(8,128)(2,1)S(1)}, bf16[48,512]{1,0:T(8,128)(2,1)S(1)}, u32[]{:S(2)}, u32[]{:S(2)}) %collective-permute-start.6) | collective-permute-done | bytes 49184 | tf_op jit(solution)/shard_map/ppermute | solution.py:17
  24.3 1.0 %template.1 = bf16[45,4096]{1,0:T(8,128)(2,1)} custom-call(bf16[45,1024]{1,0:T(8,128)(2,1)S(1)} %place.3.refs_0_, bf16[45,1024]{1,0:T(8,128)(2,1)S(1)} %place.4.refs_1_, bf16[45,1024]{1,0:T(8,128)(2,1)S(1)} %place.5.refs_2_, bf16[48,512]{1,0:T(8,128)(2,1)S(1)} %collective-permute-done.6.refs_3_), custom_call_target="tpu_custom_call" | custom-call | tf_op jit(solution)/shard_map/template/pallas_call | solution.py:204
  (1 shorter events, 0.0 us)
Async XLA Ops:
  0.0 18.5 %copy-start = (s32[512]{0:T(512)S(1)}, s32[512]{0:T(512)}, u32[]{:S(2)}) copy-start(s32[512]{0:T(512)} %param.11) | copy-start | bytes 6148
  3.8 6.7 %collective-permute-start = (f32[184,128]{1,0:T(8,128)S(1)}, f32[184,128]{1,0:T(8,128)S(1)}, u32[]{:S(2)}, u32[]{:S(2)}) collective-permute-start(f32[184,128]{1,0:T(8,128)S(1)} %local_sums.1), channel_id=1, source_target_pairs={{0,16},{1,9},{2,18},{3,11},{4,20},{5,13},{6,22},{7,15},{8,24},{9,1... | collective-permute-start | bytes 282632 | tf_op jit(solution)/shard_map/ppermute | solution.py:22
  10.5 6.6 %collective-permute-start.3 = (f32[184,128]{1,0:T(8,128)S(1)}, f32[184,128]{1,0:T(8,128)S(1)}, u32[]{:S(2)}, u32[]{:S(2)}) collective-permute-start(f32[184,128]{1,0:T(8,128)S(1)} %add.3.refs_0_), channel_id=1, source_target_pairs={{0,12},{1,21},{2,14},{3,23},{4,8},{5,17},{6,10},{7,19},{8,4},{9,29... | collective-permute-start | bytes 282632 | tf_op jit(solution)/shard_map/ppermute | solution.py:22
  13.5 4.9 %collective-permute-start.2 = (f32[184,128]{1,0:T(8,128)S(1)}, f32[184,128]{1,0:T(8,128)S(1)}, u32[]{:S(2)}, u32[]{:S(2)}) collective-permute-start(f32[184,128]{1,0:T(8,128)S(1)} %add.3.refs_0_), channel_id=1, source_target_pairs={{0,8},{1,17},{2,10},{3,19},{4,12},{5,21},{6,14},{7,23},{8,0},{9,25... | collective-permute-start | bytes 282632 | tf_op jit(solution)/shard_map/ppermute | solution.py:22
  13.9 4.6 %collective-permute-start.1 = (f32[184,128]{1,0:T(8,128)S(1)}, f32[184,128]{1,0:T(8,128)S(1)}, u32[]{:S(2)}, u32[]{:S(2)}) collective-permute-start(f32[184,128]{1,0:T(8,128)S(1)} %add.3.refs_0_), channel_id=1, source_target_pairs={{0,4},{1,5},{2,6},{3,7},{4,0},{5,1},{6,2},{7,3},{8,12},{9,13},{10,... | collective-permute-start | bytes 282632 | tf_op jit(solution)/shard_map/ppermute | solution.py:22
  18.5 4.1 %collective-permute-start.5 = (bf16[48,512]{1,0:T(8,128)(2,1)S(1)}, bf16[48,512]{1,0:T(8,128)(2,1)S(1)}, u32[]{:S(2)}, u32[]{:S(2)}) collective-permute-start(bf16[48,512]{1,0:T(8,128)(2,1)S(1)} %finish.1.compact_ref), channel_id=1, source_target_pairs={{0,3},{1,2},{2,1},{3,0},{4,7},{5,6},{6,5},{7,4},{8,11},{9,10},{10,... | collective-permute-start | bytes 147464 | tf_op jit(solution)/shard_map/ppermute | solution.py:17
  18.6 4.3 %collective-permute-start.4 = (bf16[48,512]{1,0:T(8,128)(2,1)S(1)}, bf16[48,512]{1,0:T(8,128)(2,1)S(1)}, u32[]{:S(2)}, u32[]{:S(2)}) collective-permute-start(bf16[48,512]{1,0:T(8,128)(2,1)S(1)} %finish.1.compact_ref), channel_id=1, source_target_pairs={{0,1},{1,0},{2,3},{3,2},{4,5},{5,4},{6,7},{7,6},{8,9},{9,8},{10,11... | collective-permute-start | bytes 147464 | tf_op jit(solution)/shard_map/ppermute | solution.py:17
  20.2 4.1 %collective-permute-start.6 = (bf16[48,512]{1,0:T(8,128)(2,1)S(1)}, bf16[48,512]{1,0:T(8,128)(2,1)S(1)}, u32[]{:S(2)}, u32[]{:S(2)}) collective-permute-start(bf16[48,512]{1,0:T(8,128)(2,1)S(1)} %finish.1.compact_ref), channel_id=1, source_target_pairs={{0,2},{1,3},{2,0},{3,1},{4,6},{5,7},{6,4},{7,5},{8,10},{9,11},{10,... | collective-permute-start | bytes 147464 | tf_op jit(solution)/shard_map/ppermute | solution.py:17

commit v9 on v7

--- a/solution.py
+++ b/solution.py
@@ -149,25 +149,23 @@
     )(*parts, cells.reshape(blocks, LANES))
 
 
-def dense_of(coef, compact):
+def dense_tiles(coef, compact):
     voxels = compact.shape[1]
     high = compact[coef : coef + 1].astype(jnp.float32)
     low = compact[coef + 1 : coef + 2].astype(jnp.float32)
     cells = (high * SPLIT + low).astype(jnp.int32)
-    tiles = []
     for start in range(0, GRID_DEV, TILE):
         first = max(start - (GRID_DEV - voxels), 0) // TILE * TILE
         last = min(start + TILE, voxels)
         hit = lax.broadcasted_iota(jnp.int32, (TILE, last - first), 0) + start == cells[:, first:last]
         onehot = jnp.where(hit, 1.0, 0.0).astype(jnp.bfloat16)
-        tiles.append(
-            lax.dot_general(compact[:, first:last], onehot, (((1,), (1,)), ((), ())), preferred_element_type=jnp.float32)
-        )
-    return jnp.concatenate(tiles, axis=1)[:coef].astype(jnp.bfloat16)
+        dense = lax.dot_general(compact[:, first:last], onehot, (((1,), (1,)), ((), ())), preferred_element_type=jnp.float32)
+        yield start, dense[:coef].astype(jnp.bfloat16)
 
 
 def place_kernel(coef, compact_ref, out_ref):
-    out_ref[...] = dense_of(coef, compact_ref[...])
+    for start, tile in dense_tiles(coef, compact_ref[...]):
+        out_ref[:, pl.ds(start, TILE)] = tile
 
 
 def place(coef, compact):
@@ -193,9 +191,13 @@
     copies = [write(i, ref) for i, ref in enumerate(ready)]
     for copy in copies:
         copy.start()
-    last[...] = dense_of(coef, compact_ref[...])
-    copies.append(write(len(ready), last))
-    copies[-1].start()
+    base = pl.multiple_of((index ^ order[-1]) * GRID_DEV, GRID_DEV)
+    for n, (start, tile) in enumerate(dense_tiles(coef, compact_ref[...])):
+        here = pl.ds(start, TILE)
+        last[:, here] = tile
+        there = out_ref.at[:, pl.ds(pl.multiple_of(base + start, TILE), TILE)]
+        copies.append(pltpu.make_async_copy(last.at[:, here], there, sem.at[len(ready) + n]))
+        copies[-1].start()
     for copy in copies:
         copy.wait()
 
@@ -206,7 +208,7 @@
         out_shape=jax.ShapeDtypeStruct((coef, len(order) * GRID_DEV), jnp.bfloat16),
         in_specs=[pl.BlockSpec(memory_space=pltpu.VMEM)] * len(order),
         out_specs=pl.BlockSpec(memory_space=pl.ANY),
-        scratch_shapes=[pltpu.VMEM((coef, GRID_DEV), jnp.bfloat16), pltpu.SemaphoreType.DMA((len(order),))],
+        scratch_shapes=[pltpu.VMEM((coef, GRID_DEV), jnp.bfloat16), pltpu.SemaphoreType.DMA((len(ready) + GRID_DEV // TILE,))],
         compiler_params=pltpu.CompilerParams(vmem_limit_bytes=32 << 20),
         name="template",
     )(*ready, compact)

time: 25.5 us -> 25.5 us (level)
  no operation moved by 1% of the time
where the time goes in v9:
time: 25.5 us; the launch traced here: 25.3 us
  starting transfers between devices  10 us (39%)
  waiting for transfers between devices  9.29 us (36%)
  Pallas kernels  5.96 us (23%)
    ppermute x4, starting transfers between devices, exchange_by_core(): return lax.ppermute(value, ('subj', 'slab'), pairs)  7.8 us
    ppermute x4, waiting for transfers between devices, exchange_by_core(): return lax.ppermute(value, ('subj', 'slab'), pairs)  6.83 us
    pallas_call x1, Pallas kernels, local_sums(): pl.pallas_call(functools.partial(sums_kernel, subjects, chunk), out_shape...  3.81 us
    ppermute x3, waiting for transfers between devices, exchange(): return lax.ppermute(value, axis, [(i, i ^ bit) for i in range(size)])  2.46 us
    ppermute x3, starting transfers between devices, exchange(): return lax.ppermute(value, axis, [(i, i ^ bit) for i in range(size)])  2.2 us
    pallas_call x3, Pallas kernels, place(): pl.pallas_call(functools.partial(place_kernel, coef), out_shape=pltpu.VME...  1.06 us
    pallas_call x1, Pallas kernels, template(): pl.pallas_call(functools.partial(template_kernel, coef, order), out_shape...  1.03 us
  transfers between devices with their start and end apart: 7, of which 5 were waited for; matrix products, arithmetic and copies ran while one was open for 0% of the time, Pallas kernels for 4%

profile of v9, /device:TPU:0, one launch (start us, length us, event | category | flops | bytes accessed | tf_op | source)
XLA Modules:
  0.0 25.3 jit_solution(2848299401796407975)
XLA Ops:
  0.0 0.0 copy-start
  0.0 3.8 %local_sums.1 = f32[184,128]{1,0:T(8,128)S(1)} custom-call(bf16[45,45,16,128]{3,2,1,0:T(8,128)(2,1)} %bitcast.21, bf16[45,16,128]{2,1,0:T(8,128)(2,1)} %bitcast.22, f32[16,128]{1,0:T(8,128)} %bitcast.23, s32[4]{0:T(128)} %ids_hbm.1, f32[32]{0:T(128)} %study_hbm.1), custom_call_target="tpu_custom_call" | custom-call | tf_op jit(solution)/shard_map/local_sums/pallas_call | solution.py:99
  3.8 4.1 %collective-permute-start = (f32[184,128]{1,0:T(8,128)S(1)}, f32[184,128]{1,0:T(8,128)S(1)}, u32[]{:S(2)}, u32[]{:S(2)}) collective-permute-start(f32[184,128]{1,0:T(8,128)S(1)} %local_sums.1), channel_id=1, source_target_pairs={{0,16},{1,9},{2,18},{3,11},{4,20},{5,13},{6,22},{7,15},{8,24},{9,1... | collective-permute-start | bytes 282632 | tf_op jit(solution)/shard_map/ppermute | solution.py:22
  7.9 2.6 %collective-permute-done = f32[184,128]{1,0:T(8,128)S(1)} collective-permute-done((f32[184,128]{1,0:T(8,128)S(1)}, f32[184,128]{1,0:T(8,128)S(1)}, u32[]{:S(2)}, u32[]{:S(2)}) %collective-permute-start) | collective-permute-done | bytes 94240 | tf_op jit(solution)/shard_map/ppermute | solution.py:22
  10.5 3.0 %collective-permute-start.3 = (f32[184,128]{1,0:T(8,128)S(1)}, f32[184,128]{1,0:T(8,128)S(1)}, u32[]{:S(2)}, u32[]{:S(2)}) collective-permute-start(f32[184,128]{1,0:T(8,128)S(1)} %add.3.refs_0_), channel_id=1, source_target_pairs={{0,12},{1,21},{2,14},{3,23},{4,8},{5,17},{6,10},{7,19},{8,4},{9,29... | collective-permute-start | bytes 282632 | tf_op jit(solution)/shard_map/ppermute | solution.py:22
  13.5 0.3 %collective-permute-start.2 = (f32[184,128]{1,0:T(8,128)S(1)}, f32[184,128]{1,0:T(8,128)S(1)}, u32[]{:S(2)}, u32[]{:S(2)}) collective-permute-start(f32[184,128]{1,0:T(8,128)S(1)} %add.3.refs_0_), channel_id=1, source_target_pairs={{0,8},{1,17},{2,10},{3,19},{4,12},{5,21},{6,14},{7,23},{8,0},{9,25... | collective-permute-start | bytes 282632 | tf_op jit(solution)/shard_map/ppermute | solution.py:22
  13.9 0.3 %collective-permute-start.1 = (f32[184,128]{1,0:T(8,128)S(1)}, f32[184,128]{1,0:T(8,128)S(1)}, u32[]{:S(2)}, u32[]{:S(2)}) collective-permute-start(f32[184,128]{1,0:T(8,128)S(1)} %add.3.refs_0_), channel_id=1, source_target_pairs={{0,4},{1,5},{2,6},{3,7},{4,0},{5,1},{6,2},{7,3},{8,12},{9,13},{10,... | collective-permute-start | bytes 282632 | tf_op jit(solution)/shard_map/ppermute | solution.py:22
  14.2 2.9 %collective-permute-done.3.refs_3_ = f32[184,128]{1,0:T(8,128)S(1)} collective-permute-done((f32[184,128]{1,0:T(8,128)S(1)}, f32[184,128]{1,0:T(8,128)S(1)}, u32[]{:S(2)}, u32[]{:S(2)}) %collective-permute-start.3) | collective-permute-done | bytes 94240 | tf_op jit(solution)/shard_map/ppermute | solution.py:22
  17.1 1.3 %collective-permute-done.2.refs_2_ = f32[184,128]{1,0:T(8,128)S(1)} collective-permute-done((f32[184,128]{1,0:T(8,128)S(1)}, f32[184,128]{1,0:T(8,128)S(1)}, u32[]{:S(2)}, u32[]{:S(2)}) %collective-permute-start.2) | collective-permute-done | bytes 94240 | tf_op jit(solution)/shard_map/ppermute | solution.py:22
  18.5 0.0 collective-permute-done.1.refs_1_
  18.5 0.0 copy-done
  18.5 0.1 finish.1.compact_ref
  18.5 0.1 collective-permute-start.5
  18.6 1.6 %collective-permute-start.4 = (bf16[48,512]{1,0:T(8,128)(2,1)S(1)}, bf16[48,512]{1,0:T(8,128)(2,1)S(1)}, u32[]{:S(2)}, u32[]{:S(2)}) collective-permute-start(bf16[48,512]{1,0:T(8,128)(2,1)S(1)} %finish.1.compact_ref), channel_id=1, source_target_pairs={{0,1},{1,0},{2,3},{3,2},{4,5},{5,4},{6,7},{7,6},{8,9},{9,8},{10,11... | collective-permute-start | bytes 147464 | tf_op jit(solution)/shard_map/ppermute | solution.py:17
  20.2 0.5 %collective-permute-start.6 = (bf16[48,512]{1,0:T(8,128)(2,1)S(1)}, bf16[48,512]{1,0:T(8,128)(2,1)S(1)}, u32[]{:S(2)}, u32[]{:S(2)}) collective-permute-start(bf16[48,512]{1,0:T(8,128)(2,1)S(1)} %finish.1.compact_ref), channel_id=1, source_target_pairs={{0,2},{1,3},{2,0},{3,1},{4,6},{5,7},{6,4},{7,5},{8,10},{9,11},{10,... | collective-permute-start | bytes 147464 | tf_op jit(solution)/shard_map/ppermute | solution.py:17
  20.7 0.4 %place.3.refs_0_ = bf16[45,1024]{1,0:T(8,128)(2,1)S(1)} custom-call(bf16[48,512]{1,0:T(8,128)(2,1)S(1)} %finish.1.compact_ref), custom_call_target="tpu_custom_call" | custom-call | flops 47185920 | bytes 262144 | tf_op jit(solution)/shard_map/place/pallas_call | solution.py:172
  21.1 1.5 %collective-permute-done.5.compact_ref = bf16[48,512]{1,0:T(8,128)(2,1)S(1)} collective-permute-done((bf16[48,512]{1,0:T(8,128)(2,1)S(1)}, bf16[48,512]{1,0:T(8,128)(2,1)S(1)}, u32[]{:S(2)}, u32[]{:S(2)}) %collective-permute-start.5) | collective-permute-done | bytes 49184 | tf_op jit(solution)/shard_map/ppermute | solution.py:17
  22.6 0.4 %place.5.refs_2_ = bf16[45,1024]{1,0:T(8,128)(2,1)S(1)} custom-call(bf16[48,512]{1,0:T(8,128)(2,1)S(1)} %collective-permute-done.5.compact_ref), custom_call_target="tpu_custom_call" | custom-call | flops 47185920 | bytes 262144 | tf_op jit(solution)/shard_map/place/pallas_call | solution.py:172
  22.9 0.0 collective-permute-done.4.compact_ref
  23.0 0.4 %place.4.refs_1_ = bf16[45,1024]{1,0:T(8,128)(2,1)S(1)} custom-call(bf16[48,512]{1,0:T(8,128)(2,1)S(1)} %collective-permute-done.4.compact_ref), custom_call_target="tpu_custom_call" | custom-call | flops 47185920 | bytes 262144 | tf_op jit(solution)/shard_map/place/pallas_call | solution.py:172
  23.3 1.0 %collective-permute-done.6.refs_3_ = bf16[48,512]{1,0:T(8,128)(2,1)S(1)} collective-permute-done((bf16[48,512]{1,0:T(8,128)(2,1)S(1)}, bf16[48,512]{1,0:T(8,128)(2,1)S(1)}, u32[]{:S(2)}, u32[]{:S(2)}) %collective-permute-start.6) | collective-permute-done | bytes 49184 | tf_op jit(solution)/shard_map/ppermute | solution.py:17
  24.3 1.0 %template.1 = bf16[45,4096]{1,0:T(8,128)(2,1)} custom-call(bf16[45,1024]{1,0:T(8,128)(2,1)S(1)} %place.3.refs_0_, bf16[45,1024]{1,0:T(8,128)(2,1)S(1)} %place.4.refs_1_, bf16[45,1024]{1,0:T(8,128)(2,1)S(1)} %place.5.refs_2_, bf16[48,512]{1,0:T(8,128)(2,1)S(1)} %collective-permute-done.6.refs_3_), custom_call_target="tpu_custom_call" | custom-call | tf_op jit(solution)/shard_map/template/pallas_call | solution.py:206
  (1 shorter events, 0.0 us)
Async XLA Ops:
  0.0 18.5 %copy-start = (s32[512]{0:T(512)S(1)}, s32[512]{0:T(512)}, u32[]{:S(2)}) copy-start(s32[512]{0:T(512)} %param.11) | copy-start | bytes 6148
  3.8 6.7 %collective-permute-start = (f32[184,128]{1,0:T(8,128)S(1)}, f32[184,128]{1,0:T(8,128)S(1)}, u32[]{:S(2)}, u32[]{:S(2)}) collective-permute-start(f32[184,128]{1,0:T(8,128)S(1)} %local_sums.1), channel_id=1, source_target_pairs={{0,16},{1,9},{2,18},{3,11},{4,20},{5,13},{6,22},{7,15},{8,24},{9,1... | collective-permute-start | bytes 282632 | tf_op jit(solution)/shard_map/ppermute | solution.py:22
  10.5 6.6 %collective-permute-start.3 = (f32[184,128]{1,0:T(8,128)S(1)}, f32[184,128]{1,0:T(8,128)S(1)}, u32[]{:S(2)}, u32[]{:S(2)}) collective-permute-start(f32[184,128]{1,0:T(8,128)S(1)} %add.3.refs_0_), channel_id=1, source_target_pairs={{0,12},{1,21},{2,14},{3,23},{4,8},{5,17},{6,10},{7,19},{8,4},{9,29... | collective-permute-start | bytes 282632 | tf_op jit(solution)/shard_map/ppermute | solution.py:22
  13.5 4.9 %collective-permute-start.2 = (f32[184,128]{1,0:T(8,128)S(1)}, f32[184,128]{1,0:T(8,128)S(1)}, u32[]{:S(2)}, u32[]{:S(2)}) collective-permute-start(f32[184,128]{1,0:T(8,128)S(1)} %add.3.refs_0_), channel_id=1, source_target_pairs={{0,8},{1,17},{2,10},{3,19},{4,12},{5,21},{6,14},{7,23},{8,0},{9,25... | collective-permute-start | bytes 282632 | tf_op jit(solution)/shard_map/ppermute | solution.py:22
  13.9 4.6 %collective-permute-start.1 = (f32[184,128]{1,0:T(8,128)S(1)}, f32[184,128]{1,0:T(8,128)S(1)}, u32[]{:S(2)}, u32[]{:S(2)}) collective-permute-start(f32[184,128]{1,0:T(8,128)S(1)} %add.3.refs_0_), channel_id=1, source_target_pairs={{0,4},{1,5},{2,6},{3,7},{4,0},{5,1},{6,2},{7,3},{8,12},{9,13},{10,... | collective-permute-start | bytes 282632 | tf_op jit(solution)/shard_map/ppermute | solution.py:22
  18.5 4.1 %collective-permute-start.5 = (bf16[48,512]{1,0:T(8,128)(2,1)S(1)}, bf16[48,512]{1,0:T(8,128)(2,1)S(1)}, u32[]{:S(2)}, u32[]{:S(2)}) collective-permute-start(bf16[48,512]{1,0:T(8,128)(2,1)S(1)} %finish.1.compact_ref), channel_id=1, source_target_pairs={{0,3},{1,2},{2,1},{3,0},{4,7},{5,6},{6,5},{7,4},{8,11},{9,10},{10,... | collective-permute-start | bytes 147464 | tf_op jit(solution)/shard_map/ppermute | solution.py:17
  18.6 4.3 %collective-permute-start.4 = (bf16[48,512]{1,0:T(8,128)(2,1)S(1)}, bf16[48,512]{1,0:T(8,128)(2,1)S(1)}, u32[]{:S(2)}, u32[]{:S(2)}) collective-permute-start(bf16[48,512]{1,0:T(8,128)(2,1)S(1)} %finish.1.compact_ref), channel_id=1, source_target_pairs={{0,1},{1,0},{2,3},{3,2},{4,5},{5,4},{6,7},{7,6},{8,9},{9,8},{10,11... | collective-permute-start | bytes 147464 | tf_op jit(solution)/shard_map/ppermute | solution.py:17
  20.2 4.1 %collective-permute-start.6 = (bf16[48,512]{1,0:T(8,128)(2,1)S(1)}, bf16[48,512]{1,0:T(8,128)(2,1)S(1)}, u32[]{:S(2)}, u32[]{:S(2)}) collective-permute-start(bf16[48,512]{1,0:T(8,128)(2,1)S(1)} %finish.1.compact_ref), channel_id=1, source_target_pairs={{0,2},{1,3},{2,0},{3,1},{4,6},{5,7},{6,4},{7,5},{8,10},{9,11},{10,... | collective-permute-start | bytes 147464 | tf_op jit(solution)/shard_map/ppermute | solution.py:17
